TPU v7x, 32 devices: a whole 2x2x4 slice. The times are simulated.
32 devices in a mesh: section: 4 (over y, x), depth: 8 (over z, core).
Axes of the slice: x: 2, y: 2, z: 4, core: 2. Of those that a mesh axis runs over, the one named last changes fastest.
Arguments:
- activations: float32 [4, 4, 16, 64, 256], P('section', None, 'depth'), may hold values from -6 to 6
- filters: float32 [4, 27, 64, 64], P('section'), may hold values from -0.15625 to 0.15625
- cotangent: float32 [4, 16, 64, 256], P(None, 'depth'), may hold values from -6 to 6
Outputs:
- input_grads: float32 [4, 4, 16, 64, 256], P('section', None, 'depth')
- filter_grads: float32 [4, 27, 64, 64], P('section')
All inputs are finite; a program needn't handle non-finite values.
Results may differ from a plain program's by a relative error of at most 0.0003.
Values sent between devices are 32-bit elements; how exact they have to be, the bound alone decides.
A program may use at most 128 MiB of HBM per device.

v0:
```python
import math

import jax
import jax.numpy as jnp
from jax import lax
from jax.sharding import PartitionSpec as P

H = 16
W = 16


def padded_2(cells, sides, width):
    for axis, dim in sides:
        count = lax.axis_size(axis)
        ends = count - 1
        head = lax.slice_in_dim(cells, 0, width, axis=dim)
        tail = lax.slice_in_dim(cells, cells.shape[dim] - width, cells.shape[dim], axis=dim)
        cells = jnp.concatenate(
            [
                lax.ppermute(tail, axis, [(i, (i + 1) % count) for i in range(ends)]),
                cells,
                lax.ppermute(head, axis, [((i + 1) % count, i) for i in range(ends)]),
            ],
            axis=dim,
        )
    return cells


def shifted(shard, axis, by):
    size = lax.axis_size(axis)
    pairs = [(i, i + by) for i in range(size) if 0 <= i + by < size]
    return lax.ppermute(shard, axis, pairs)


def neighbours(extended, height, breadth):
    planes, channels, columns = extended.shape
    volume_grid = extended.reshape(planes, channels, height, breadth)
    padded = jnp.pad(volume_grid, ((0, 0), (0, 0), (1, 1), (1, 1)))
    pieces = [
        padded[:, :, row_shift : row_shift + height, col_shift : col_shift + breadth]
        for row_shift in range(3)
        for col_shift in range(3)
    ]
    return jnp.stack(pieces, axis=1).reshape(planes, 9, channels, columns)


def apply_taps(patches, kernel_taps, count):
    result = jnp.zeros((count, kernel_taps.shape[2], patches.shape[3]), jnp.float32)
    for plane_shift in range(3):
        result = result + jnp.einsum(
            "koc,dkcp->dop",
            kernel_taps[plane_shift],
            patches[plane_shift : plane_shift + count],
            precision=lax.Precision.HIGHEST,
        )
    return result


def silu_slope(preact):
    sigmoid_value = jax.nn.sigmoid(preact)
    return sigmoid_value * (1.0 + preact * (1.0 - sigmoid_value))


def per_device(activations, filters, cotangent):
    sections = lax.axis_size("section")
    section_index = lax.axis_index("section")
    micro_count = activations.shape[1]
    slab_planes = activations.shape[2]
    channels = activations.shape[3]
    columns = activations.shape[4]
    height = H
    breadth = W
    kernel_taps = filters[0].reshape(3, 9, channels, channels)
    flipped = jnp.flip(filters[0], 0).transpose(0, 2, 1).reshape(3, 9, channels, channels)
    extended_all = padded_2(activations[0], (("depth", 1),), 1)

    def prepare(extended_one):
        patch_one = neighbours(extended_one, height, breadth)
        return (patch_one, silu_slope(apply_taps(patch_one, kernel_taps, slab_planes)))

    patch_store, slope_store = jax.vmap(prepare)(extended_all)

    def advance(tick_count, state_carry):
        incoming, grad_store, filter_sum = state_carry
        micro_index = tick_count - (sections - 1 - section_index)
        active = (micro_index >= 0) & (micro_index < micro_count)
        slot_index = jnp.clip(micro_index, 0, micro_count - 1)
        top_grad = lax.dynamic_index_in_dim(cotangent, slot_index, 0, keepdims=False)
        upstream = jnp.where(section_index == sections - 1, top_grad, incoming)
        patches = lax.dynamic_index_in_dim(patch_store, slot_index, 0, keepdims=False)
        inner_grad = upstream * lax.dynamic_index_in_dim(slope_store, slot_index, 0, keepdims=False)
        slopes = padded_2(inner_grad, (("depth", 0),), 1)
        offset = 0
        backward = apply_taps(neighbours(slopes, height, breadth), flipped, slab_planes)
        own_slopes = slopes[1 : 1 + slab_planes]
        pieces = [
            jnp.einsum(
                "dop,dkcp->koc",
                own_slopes,
                patches[offset + plane_shift : offset + plane_shift + slab_planes],
                precision=lax.Precision.HIGHEST,
            )
            for plane_shift in range(3)
        ]
        filter_term = jnp.where(active, jnp.stack(pieces).reshape(27, channels, channels), 0.0)
        grad_store = jnp.where(
            active, lax.dynamic_update_index_in_dim(grad_store, backward, slot_index, 0), grad_store
        )
        filter_sum = filter_sum + filter_term
        passed = shifted(backward, "section", -1)
        return (passed, grad_store, filter_sum)

    start = (
        jnp.zeros((slab_planes, channels, columns), jnp.float32),
        jnp.zeros((micro_count, slab_planes, channels, columns), jnp.float32),
        jnp.zeros((27, channels, channels), jnp.float32),
    )
    passed, grad_store, filter_sum = lax.fori_loop(0, micro_count + sections - 1, advance, start)
    summed = lax.psum(filter_sum, "depth")
    scaling = 1.0 / math.sqrt(micro_count * slab_planes * lax.axis_size("depth") * height * breadth)
    return (grad_store[None], (summed * scaling)[None])


def solution(mesh):
    return jax.shard_map(
        per_device,
        mesh=mesh,
        in_specs=(
            P("section", None, "depth", None, None),
            P("section", None, None, None),
            P(None, "depth", None, None),
        ),
        out_specs=(P("section", None, "depth", None, None), P("section", None, None, None)),
        check_vma=False,
    )
```

profile of v0, /device:TPU:1, one launch (start us, length us, event | category | flops | bytes accessed | tf_op | source)
XLA Modules:
  0.0 386.2 jit_solution(3482253026435452872)
XLA Ops:
  11.0 4.6 %collective-permute-start.3 = (f32[4,1,64,256]{3,2,0,1:T(8,128)}, f32[4,1,64,256]{3,2,0,1:T(8,128)}, u32[]{:S(2)}, u32[]{:S(2)}) collective-permute-start(f32[4,1,64,256]{3,2,0,1:T(8,128)} %get-tuple-element.325), channel_id=1, source_target_pairs={{0,1},{1,2},{2,3},{3,4},{4,5},{5,6},{6,7},{8,9},{9,10},{10,11},{11... | collective-permute-start | bytes 786440 | tf_op jit(solution)/shard_map/ppermute | solution.py:20
  24.2 5.9 %fusion.48 = (f32[4,4,64,16,16]{2,4,3,1,0:T(8,128)}, f32[4,4,64,16,16]{2,4,3,1,0:T(8,128)}, f32[4,4,64,16,16]{2,4,3,1,0:T(8,128)}, f32[4,4,64,16,16]{2,4,3,1,0:T...) fusion(f32[4,4,64,18,18]{2,4,3,1,0:T(8,128)S(1)} %select_maximu, ...), kind=kLoop, calls=%fused_computation.96 | loop fusion | bytes 16777216 | tf_op jit(solution)/shard_map/vmap()/slice | solution.py:40
  30.1 2.2 copy.46
  32.3 3.2 copy.45
  35.4 3.2 copy.44
  38.7 3.2 copy.43
  41.8 3.2 copy.42
  45.1 3.2 copy.41
  48.2 3.2 copy.40
  51.4 3.2 copy.39
  60.5 3.4 convolution_bitcast_fusion.3
  63.9 3.4 convolution_bitcast_fusion.4
  67.3 4.5 %add_multiply_fusion = f32[4,2,64,256]{3,2,1,0:T(8,128)} fusion(f32[4,2,256,64]{2,3,1,0:T(8,128)S(1)} %convolution_bitcast_fusion.3, f32[4,2,256,64]{2,3,1,0:T(8,128)S(1)} %convolution_bitcast_fusion.4, f32[4,4,9,64,256]{4,3,2,1,0:T(8,128)S(1)} %constant_dynamic-update-slice_fusion.1, f32[1,27,64,64]{3,2,1,0:T(8,128)S(1)} %copy-done.8), kind=kOutput, calls=%fused_computation.79 | convolution fusion | flops 907149312 | bytes 11304960 | tf_op jit(solution)/shard_map/vmap(koc,dkcp->dop)/dot_general | solution.py:50
  73.2 245.0 %while.20 = (s32[]{:T(128)}, f32[2,64,256]{2,1,0:T(8,128)}, f32[4,2,64,256]{3,2,1,0:T(8,128)}, f32[27,64,64]{1,2,0:T(8,128)S(1)}, pred[]{:T(512)}, /*index=5*/s3...) while((s32[]{:T(128)}, f32[2,64,256]{2,1,0:T(8,128)}, ...), condition=%wide.region_1.2_spmd.clone, body=%wide.region_0.1_spmd.clone.sunk | while | flops 1359802368 | bytes 42467708 | solution.py:118
  78.2 3.6 collective-permute-start.1
  81.9 2.2 constant_dynamic-slice_fusion.8
  91.6 2.5 convolution_bitcast_fusion.8
  94.1 2.5 convolution_bitcast_fusion.9
  96.6 4.1 %fusion.96 = (f32[4,2,64,256]{3,2,1,0:T(8,128)}, f32[2,256,64]{1,2,0:T(8,128)S(1)}) fusion(f32[4,2,64,256]{3,2,1,0:T(8,128)} %get-tuple-element.430, s32[]{:T(128)S(6)} %min.13, pred[]{:T(512)S(6)} %and.33, f32[2,256,64]{1,2,0:T(8,128)S(1)} %convolution_bitcast_fusion.8, f32[2,256,64]{1,2,0:T(8,128)S(1)} %convolution_bitcast_fusion.9, ...), kind=kOutput, calls=%fused_computation.53.clone.1 | convolution fusion | flops 226590720 | bytes 3309573 | tf_op jit(solution)/shard_map/while/body/eval_jaxpr/koc,dkcp->dop/dot_general | solution.py:50
  102.3 5.7 %collective-permute-done.2 = f32[2,64,256]{2,1,0:T(8,128)} collective-permute-done((f32[2,64,256]{2,1,0:T(8,128)S(1)}, f32[2,64,256]{2,1,0:T(8,128)}, u32[]{:S(2)}, u32[]{:S(2)}) %collective-permute-start.2) | collective-permute-done | bytes 131104 | tf_op jit(solution)/shard_map/while/body/eval_jaxpr/ppermute | solution.py:32
  111.1 2.3 collective-permute-start
  113.4 3.3 collective-permute-start.1
  116.6 2.2 constant_dynamic-slice_fusion.8
  126.3 2.5 convolution_bitcast_fusion.8
  128.9 2.5 convolution_bitcast_fusion.9
  131.4 4.1 %fusion.96 = (f32[4,2,64,256]{3,2,1,0:T(8,128)}, f32[2,256,64]{1,2,0:T(8,128)S(1)}) fusion(f32[4,2,64,256]{3,2,1,0:T(8,128)} %get-tuple-element.430, s32[]{:T(128)S(6)} %min.13, pred[]{:T(512)S(6)} %and.33, f32[2,256,64]{1,2,0:T(8,128)S(1)} %convolution_bitcast_fusion.8, f32[2,256,64]{1,2,0:T(8,128)S(1)} %convolution_bitcast_fusion.9, ...), kind=kOutput, calls=%fused_computation.53.clone.1 | convolution fusion | flops 226590720 | bytes 3309573 | tf_op jit(solution)/shard_map/while/body/eval_jaxpr/koc,dkcp->dop/dot_general | solution.py:50
  137.0 6.5 %collective-permute-done.2 = f32[2,64,256]{2,1,0:T(8,128)} collective-permute-done((f32[2,64,256]{2,1,0:T(8,128)S(1)}, f32[2,64,256]{2,1,0:T(8,128)}, u32[]{:S(2)}, u32[]{:S(2)}) %collective-permute-start.2) | collective-permute-done | bytes 131104 | tf_op jit(solution)/shard_map/while/body/eval_jaxpr/ppermute | solution.py:32
  146.6 2.3 collective-permute-start
  148.9 3.3 collective-permute-start.1
  152.2 2.2 constant_dynamic-slice_fusion.8
  161.9 2.5 convolution_bitcast_fusion.8
  164.4 2.5 convolution_bitcast_fusion.9
  167.0 4.1 %fusion.96 = (f32[4,2,64,256]{3,2,1,0:T(8,128)}, f32[2,256,64]{1,2,0:T(8,128)S(1)}) fusion(f32[4,2,64,256]{3,2,1,0:T(8,128)} %get-tuple-element.430, s32[]{:T(128)S(6)} %min.13, pred[]{:T(512)S(6)} %and.33, f32[2,256,64]{1,2,0:T(8,128)S(1)} %convolution_bitcast_fusion.8, f32[2,256,64]{1,2,0:T(8,128)S(1)} %convolution_bitcast_fusion.9, ...), kind=kOutput, calls=%fused_computation.53.clone.1 | convolution fusion | flops 226590720 | bytes 3309573 | tf_op jit(solution)/shard_map/while/body/eval_jaxpr/koc,dkcp->dop/dot_general | solution.py:50
  172.6 6.4 %collective-permute-done.2 = f32[2,64,256]{2,1,0:T(8,128)} collective-permute-done((f32[2,64,256]{2,1,0:T(8,128)S(1)}, f32[2,64,256]{2,1,0:T(8,128)}, u32[]{:S(2)}, u32[]{:S(2)}) %collective-permute-start.2) | collective-permute-done | bytes 131104 | tf_op jit(solution)/shard_map/while/body/eval_jaxpr/ppermute | solution.py:32
  182.1 2.5 collective-permute-start
  184.6 3.0 collective-permute-start.1
  187.7 2.2 constant_dynamic-slice_fusion.8
  197.4 2.5 convolution_bitcast_fusion.8
  199.9 2.5 convolution_bitcast_fusion.9
  202.4 4.1 %fusion.96 = (f32[4,2,64,256]{3,2,1,0:T(8,128)}, f32[2,256,64]{1,2,0:T(8,128)S(1)}) fusion(f32[4,2,64,256]{3,2,1,0:T(8,128)} %get-tuple-element.430, s32[]{:T(128)S(6)} %min.13, pred[]{:T(512)S(6)} %and.33, f32[2,256,64]{1,2,0:T(8,128)S(1)} %convolution_bitcast_fusion.8, f32[2,256,64]{1,2,0:T(8,128)S(1)} %convolution_bitcast_fusion.9, ...), kind=kOutput, calls=%fused_computation.53.clone.1 | convolution fusion | flops 226590720 | bytes 3309573 | tf_op jit(solution)/shard_map/while/body/eval_jaxpr/koc,dkcp->dop/dot_general | solution.py:50
  208.0 6.1 %collective-permute-done.2 = f32[2,64,256]{2,1,0:T(8,128)} collective-permute-done((f32[2,64,256]{2,1,0:T(8,128)S(1)}, f32[2,64,256]{2,1,0:T(8,128)}, u32[]{:S(2)}, u32[]{:S(2)}) %collective-permute-start.2) | collective-permute-done | bytes 131104 | tf_op jit(solution)/shard_map/while/body/eval_jaxpr/ppermute | solution.py:32
  217.2 2.8 collective-permute-start
  220.0 2.8 collective-permute-start.1
  222.8 2.2 constant_dynamic-slice_fusion.8
  232.5 2.5 convolution_bitcast_fusion.8
  235.0 2.5 convolution_bitcast_fusion.9
  237.5 4.1 %fusion.96 = (f32[4,2,64,256]{3,2,1,0:T(8,128)}, f32[2,256,64]{1,2,0:T(8,128)S(1)}) fusion(f32[4,2,64,256]{3,2,1,0:T(8,128)} %get-tuple-element.430, s32[]{:T(128)S(6)} %min.13, pred[]{:T(512)S(6)} %and.33, f32[2,256,64]{1,2,0:T(8,128)S(1)} %convolution_bitcast_fusion.8, f32[2,256,64]{1,2,0:T(8,128)S(1)} %convolution_bitcast_fusion.9, ...), kind=kOutput, calls=%fused_computation.53.clone.1 | convolution fusion | flops 226590720 | bytes 3309573 | tf_op jit(solution)/shard_map/while/body/eval_jaxpr/koc,dkcp->dop/dot_general | solution.py:50
  243.2 5.8 %collective-permute-done.2 = f32[2,64,256]{2,1,0:T(8,128)} collective-permute-done((f32[2,64,256]{2,1,0:T(8,128)S(1)}, f32[2,64,256]{2,1,0:T(8,128)}, u32[]{:S(2)}, u32[]{:S(2)}) %collective-permute-start.2) | collective-permute-done | bytes 131104 | tf_op jit(solution)/shard_map/while/body/eval_jaxpr/ppermute | solution.py:32
  252.1 3.0 collective-permute-start
  255.1 2.5 collective-permute-start.1
  257.6 2.2 constant_dynamic-slice_fusion.8
  267.3 2.5 convolution_bitcast_fusion.8
  269.9 2.5 convolution_bitcast_fusion.9
  272.4 4.1 %fusion.96 = (f32[4,2,64,256]{3,2,1,0:T(8,128)}, f32[2,256,64]{1,2,0:T(8,128)S(1)}) fusion(f32[4,2,64,256]{3,2,1,0:T(8,128)} %get-tuple-element.430, s32[]{:T(128)S(6)} %min.13, pred[]{:T(512)S(6)} %and.33, f32[2,256,64]{1,2,0:T(8,128)S(1)} %convolution_bitcast_fusion.8, f32[2,256,64]{1,2,0:T(8,128)S(1)} %convolution_bitcast_fusion.9, ...), kind=kOutput, calls=%fused_computation.53.clone.1 | convolution fusion | flops 226590720 | bytes 3309573 | tf_op jit(solution)/shard_map/while/body/eval_jaxpr/koc,dkcp->dop/dot_general | solution.py:50
  278.0 5.6 %collective-permute-done.2 = f32[2,64,256]{2,1,0:T(8,128)} collective-permute-done((f32[2,64,256]{2,1,0:T(8,128)S(1)}, f32[2,64,256]{2,1,0:T(8,128)}, u32[]{:S(2)}, u32[]{:S(2)}) %collective-permute-start.2) | collective-permute-done | bytes 131104 | tf_op jit(solution)/shard_map/while/body/eval_jaxpr/ppermute | solution.py:32
  286.7 3.3 collective-permute-start
  290.0 2.3 collective-permute-start.1
  292.3 2.3 constant_dynamic-slice_fusion.8
  302.0 2.5 convolution_bitcast_fusion.8
  304.6 2.5 convolution_bitcast_fusion.9
  307.1 4.1 %fusion.96 = (f32[4,2,64,256]{3,2,1,0:T(8,128)}, f32[2,256,64]{1,2,0:T(8,128)S(1)}) fusion(f32[4,2,64,256]{3,2,1,0:T(8,128)} %get-tuple-element.430, s32[]{:T(128)S(6)} %min.13, pred[]{:T(512)S(6)} %and.33, f32[2,256,64]{1,2,0:T(8,128)S(1)} %convolution_bitcast_fusion.8, f32[2,256,64]{1,2,0:T(8,128)S(1)} %convolution_bitcast_fusion.9, ...), kind=kOutput, calls=%fused_computation.53.clone.1 | convolution fusion | flops 226590720 | bytes 3309573 | tf_op jit(solution)/shard_map/while/body/eval_jaxpr/koc,dkcp->dop/dot_general | solution.py:50
  312.7 5.5 %collective-permute-done.2 = f32[2,64,256]{2,1,0:T(8,128)} collective-permute-done((f32[2,64,256]{2,1,0:T(8,128)S(1)}, f32[2,64,256]{2,1,0:T(8,128)}, u32[]{:S(2)}, u32[]{:S(2)}) %collective-permute-start.2) | collective-permute-done | bytes 131104 | tf_op jit(solution)/shard_map/while/body/eval_jaxpr/ppermute | solution.py:32
  319.5 57.7 %all-reduce.4.cloned.1.call-done = f32[27,64,64]{2,1,0:T(8,128)} async-done(((f32[27,64,64]{2,1,0:T(8,128)}), f32[27,64,64]{2,1,0:T(8,128)}) %all-reduce.4.cloned.1.call-update) | async-done | bytes 442384 | tf_op jit(solution)/shard_map/psum | solution.py:119
  377.1 2.2 multiply_bitcast_fusion
  (220 shorter events, 106.1 us)
Async XLA Ops:
  7.2 9.9 %copy-start.7 = (f32[1,27,64,64]{3,2,1,0:T(8,128)S(1)}, f32[1,27,64,64]{3,2,1,0:T(8,128)}, u32[]{:S(2)}) copy-start(f32[1,27,64,64]{3,2,1,0:T(8,128)} %param.6) | copy-start | bytes 1327108
  7.2 370.0 %all-reduce.4.cloned.1.call-start = ((), (), s32[]{:S(2)}) async-start(), calls=%async_computation | async-start | bytes 1769472 | tf_op jit(solution)/shard_map/psum | solution.py:119
  9.1 10.4 %collective-permute-start.4 = (f32[4,1,64,256]{3,2,0,1:T(8,128)S(1)}, f32[4,1,64,256]{3,2,0,1:T(8,128)}, u32[]{:S(2)}, u32[]{:S(2)}) collective-permute-start(f32[4,1,64,256]{3,2,0,1:T(8,128)S(1)} %get-tuple-element.326), channel_id=1, source_target_pairs={{1,0},{2,1},{3,2},{4,3},{5,4},{6,5},{7,6},{9,8},{10,9},{11,10},{12... | collective-permute-start | bytes 786440 | tf_op jit(solution)/shard_map/ppermute | solution.py:22
  11.0 9.6 %collective-permute-start.3 = (f32[4,1,64,256]{3,2,0,1:T(8,128)}, f32[4,1,64,256]{3,2,0,1:T(8,128)}, u32[]{:S(2)}, u32[]{:S(2)}) collective-permute-start(f32[4,1,64,256]{3,2,0,1:T(8,128)} %get-tuple-element.325), channel_id=1, source_target_pairs={{0,1},{1,2},{2,3},{3,4},{4,5},{5,6},{6,7},{8,9},{9,10},{10,11},{11... | collective-permute-start | bytes 786440 | tf_op jit(solution)/shard_map/ppermute | solution.py:20
  54.6 2.9 copy-start.6
  54.6 3.0 copy-start.5
  56.1 1.7 copy-start.1
  57.5 1.6 copy-start.4
  57.6 1.6 copy-start.3
  57.7 1.8 copy-start.2
  59.2 1.2 copy-start.8
  60.5 6.8 %copy-start = (f32[4,4,9,64,256]{4,3,2,1,0:T(8,128)}, f32[4,4,9,64,256]{4,3,2,1,0:T(8,128)S(1)}, u32[]{:S(2)}) copy-start(f32[4,4,9,64,256]{4,3,2,1,0:T(8,128)S(1)} %constant_dynamic-update-slice_fusion.1) | copy-start | bytes 28311556
  76.3 12.9 %collective-permute-start = (f32[1,64,256]{1,2,0:T(8,128)}, f32[1,64,256]{1,2,0:T(8,128)}, u32[]{:S(2)}, u32[]{:S(2)}) collective-permute-start(f32[1,64,256]{1,2,0:T(8,128)} %get-tuple-element.402), channel_id=1, source_target_pairs={{1,0},{2,1},{3,2},{4,3},{5,4},{6,5},{7,6},{9,8},{10,9},{11,10},{12... | collective-permute-start | bytes 196616 | tf_op jit(solution)/shard_map/while/body/eval_jaxpr/ppermute | solution.py:22
  78.2 11.0 %collective-permute-start.1 = (f32[1,64,256]{1,2,0:T(8,128)}, f32[1,64,256]{1,2,0:T(8,128)}, u32[]{:S(2)}, u32[]{:S(2)}) collective-permute-start(f32[1,64,256]{1,2,0:T(8,128)} %get-tuple-element.403), channel_id=1, source_target_pairs={{0,1},{1,2},{2,3},{3,4},{4,5},{5,6},{6,7},{8,9},{9,10},{10,11},{11... | collective-permute-start | bytes 196616 | tf_op jit(solution)/shard_map/while/body/eval_jaxpr/ppermute | solution.py:20
  100.7 7.3 %collective-permute-start.2 = (f32[2,64,256]{2,1,0:T(8,128)S(1)}, f32[2,64,256]{2,1,0:T(8,128)}, u32[]{:S(2)}, u32[]{:S(2)}) collective-permute-start(f32[2,64,256]{2,1,0:T(8,128)S(1)} %bitcast.307), channel_id=1, source_target_pairs={{8,0},{16,8},{24,16},{9,1},{17,9},{25,17},{10,2},{18,10},{26,18},{... | collective-permute-start | bytes 393224 | tf_op jit(solution)/shard_map/while/body/eval_jaxpr/ppermute | solution.py:32
  111.1 12.9 %collective-permute-start = (f32[1,64,256]{1,2,0:T(8,128)}, f32[1,64,256]{1,2,0:T(8,128)}, u32[]{:S(2)}, u32[]{:S(2)}) collective-permute-start(f32[1,64,256]{1,2,0:T(8,128)} %get-tuple-element.402), channel_id=1, source_target_pairs={{1,0},{2,1},{3,2},{4,3},{5,4},{6,5},{7,6},{9,8},{10,9},{11,10},{12... | collective-permute-start | bytes 196616 | tf_op jit(solution)/shard_map/while/body/eval_jaxpr/ppermute | solution.py:22
  113.4 10.6 %collective-permute-start.1 = (f32[1,64,256]{1,2,0:T(8,128)}, f32[1,64,256]{1,2,0:T(8,128)}, u32[]{:S(2)}, u32[]{:S(2)}) collective-permute-start(f32[1,64,256]{1,2,0:T(8,128)} %get-tuple-element.403), channel_id=1, source_target_pairs={{0,1},{1,2},{2,3},{3,4},{4,5},{5,6},{6,7},{8,9},{9,10},{10,11},{11... | collective-permute-start | bytes 196616 | tf_op jit(solution)/shard_map/while/body/eval_jaxpr/ppermute | solution.py:20
  135.5 8.1 %collective-permute-start.2 = (f32[2,64,256]{2,1,0:T(8,128)S(1)}, f32[2,64,256]{2,1,0:T(8,128)}, u32[]{:S(2)}, u32[]{:S(2)}) collective-permute-start(f32[2,64,256]{2,1,0:T(8,128)S(1)} %bitcast.307), channel_id=1, source_target_pairs={{8,0},{16,8},{24,16},{9,1},{17,9},{25,17},{10,2},{18,10},{26,18},{... | collective-permute-start | bytes 393224 | tf_op jit(solution)/shard_map/while/body/eval_jaxpr/ppermute | solution.py:32
  146.6 12.9 %collective-permute-start = (f32[1,64,256]{1,2,0:T(8,128)}, f32[1,64,256]{1,2,0:T(8,128)}, u32[]{:S(2)}, u32[]{:S(2)}) collective-permute-start(f32[1,64,256]{1,2,0:T(8,128)} %get-tuple-element.402), channel_id=1, source_target_pairs={{1,0},{2,1},{3,2},{4,3},{5,4},{6,5},{7,6},{9,8},{10,9},{11,10},{12... | collective-permute-start | bytes 196616 | tf_op jit(solution)/shard_map/while/body/eval_jaxpr/ppermute | solution.py:22
  148.9 10.6 %collective-permute-start.1 = (f32[1,64,256]{1,2,0:T(8,128)}, f32[1,64,256]{1,2,0:T(8,128)}, u32[]{:S(2)}, u32[]{:S(2)}) collective-permute-start(f32[1,64,256]{1,2,0:T(8,128)} %get-tuple-element.403), channel_id=1, source_target_pairs={{0,1},{1,2},{2,3},{3,4},{4,5},{5,6},{6,7},{8,9},{9,10},{10,11},{11... | collective-permute-start | bytes 196616 | tf_op jit(solution)/shard_map/while/body/eval_jaxpr/ppermute | solution.py:20
  171.1 8.0 %collective-permute-start.2 = (f32[2,64,256]{2,1,0:T(8,128)S(1)}, f32[2,64,256]{2,1,0:T(8,128)}, u32[]{:S(2)}, u32[]{:S(2)}) collective-permute-start(f32[2,64,256]{2,1,0:T(8,128)S(1)} %bitcast.307), channel_id=1, source_target_pairs={{8,0},{16,8},{24,16},{9,1},{17,9},{25,17},{10,2},{18,10},{26,18},{... | collective-permute-start | bytes 393224 | tf_op jit(solution)/shard_map/while/body/eval_jaxpr/ppermute | solution.py:32
  182.1 12.9 %collective-permute-start = (f32[1,64,256]{1,2,0:T(8,128)}, f32[1,64,256]{1,2,0:T(8,128)}, u32[]{:S(2)}, u32[]{:S(2)}) collective-permute-start(f32[1,64,256]{1,2,0:T(8,128)} %get-tuple-element.402), channel_id=1, source_target_pairs={{1,0},{2,1},{3,2},{4,3},{5,4},{6,5},{7,6},{9,8},{10,9},{11,10},{12... | collective-permute-start | bytes 196616 | tf_op jit(solution)/shard_map/while/body/eval_jaxpr/ppermute | solution.py:22
  184.6 10.3 %collective-permute-start.1 = (f32[1,64,256]{1,2,0:T(8,128)}, f32[1,64,256]{1,2,0:T(8,128)}, u32[]{:S(2)}, u32[]{:S(2)}) collective-permute-start(f32[1,64,256]{1,2,0:T(8,128)} %get-tuple-element.403), channel_id=1, source_target_pairs={{0,1},{1,2},{2,3},{3,4},{4,5},{5,6},{6,7},{8,9},{9,10},{10,11},{11... | collective-permute-start | bytes 196616 | tf_op jit(solution)/shard_map/while/body/eval_jaxpr/ppermute | solution.py:20
  206.5 7.6 %collective-permute-start.2 = (f32[2,64,256]{2,1,0:T(8,128)S(1)}, f32[2,64,256]{2,1,0:T(8,128)}, u32[]{:S(2)}, u32[]{:S(2)}) collective-permute-start(f32[2,64,256]{2,1,0:T(8,128)S(1)} %bitcast.307), channel_id=1, source_target_pairs={{8,0},{16,8},{24,16},{9,1},{17,9},{25,17},{10,2},{18,10},{26,18},{... | collective-permute-start | bytes 393224 | tf_op jit(solution)/shard_map/while/body/eval_jaxpr/ppermute | solution.py:32
  217.2 12.9 %collective-permute-start = (f32[1,64,256]{1,2,0:T(8,128)}, f32[1,64,256]{1,2,0:T(8,128)}, u32[]{:S(2)}, u32[]{:S(2)}) collective-permute-start(f32[1,64,256]{1,2,0:T(8,128)} %get-tuple-element.402), channel_id=1, source_target_pairs={{1,0},{2,1},{3,2},{4,3},{5,4},{6,5},{7,6},{9,8},{10,9},{11,10},{12... | collective-permute-start | bytes 196616 | tf_op jit(solution)/shard_map/while/body/eval_jaxpr/ppermute | solution.py:22
  220.0 10.1 %collective-permute-start.1 = (f32[1,64,256]{1,2,0:T(8,128)}, f32[1,64,256]{1,2,0:T(8,128)}, u32[]{:S(2)}, u32[]{:S(2)}) collective-permute-start(f32[1,64,256]{1,2,0:T(8,128)} %get-tuple-element.403), channel_id=1, source_target_pairs={{0,1},{1,2},{2,3},{3,4},{4,5},{5,6},{6,7},{8,9},{9,10},{10,11},{11... | collective-permute-start | bytes 196616 | tf_op jit(solution)/shard_map/while/body/eval_jaxpr/ppermute | solution.py:20
  241.6 7.4 %collective-permute-start.2 = (f32[2,64,256]{2,1,0:T(8,128)S(1)}, f32[2,64,256]{2,1,0:T(8,128)}, u32[]{:S(2)}, u32[]{:S(2)}) collective-permute-start(f32[2,64,256]{2,1,0:T(8,128)S(1)} %bitcast.307), channel_id=1, source_target_pairs={{8,0},{16,8},{24,16},{9,1},{17,9},{25,17},{10,2},{18,10},{26,18},{... | collective-permute-start | bytes 393224 | tf_op jit(solution)/shard_map/while/body/eval_jaxpr/ppermute | solution.py:32
  252.1 12.9 %collective-permute-start = (f32[1,64,256]{1,2,0:T(8,128)}, f32[1,64,256]{1,2,0:T(8,128)}, u32[]{:S(2)}, u32[]{:S(2)}) collective-permute-start(f32[1,64,256]{1,2,0:T(8,128)} %get-tuple-element.402), channel_id=1, source_target_pairs={{1,0},{2,1},{3,2},{4,3},{5,4},{6,5},{7,6},{9,8},{10,9},{11,10},{12... | collective-permute-start | bytes 196616 | tf_op jit(solution)/shard_map/while/body/eval_jaxpr/ppermute | solution.py:22
  255.1 9.8 %collective-permute-start.1 = (f32[1,64,256]{1,2,0:T(8,128)}, f32[1,64,256]{1,2,0:T(8,128)}, u32[]{:S(2)}, u32[]{:S(2)}) collective-permute-start(f32[1,64,256]{1,2,0:T(8,128)} %get-tuple-element.403), channel_id=1, source_target_pairs={{0,1},{1,2},{2,3},{3,4},{4,5},{5,6},{6,7},{8,9},{9,10},{10,11},{11... | collective-permute-start | bytes 196616 | tf_op jit(solution)/shard_map/while/body/eval_jaxpr/ppermute | solution.py:20
  276.5 7.2 %collective-permute-start.2 = (f32[2,64,256]{2,1,0:T(8,128)S(1)}, f32[2,64,256]{2,1,0:T(8,128)}, u32[]{:S(2)}, u32[]{:S(2)}) collective-permute-start(f32[2,64,256]{2,1,0:T(8,128)S(1)} %bitcast.307), channel_id=1, source_target_pairs={{8,0},{16,8},{24,16},{9,1},{17,9},{25,17},{10,2},{18,10},{26,18},{... | collective-permute-start | bytes 393224 | tf_op jit(solution)/shard_map/while/body/eval_jaxpr/ppermute | solution.py:32
  286.7 12.9 %collective-permute-start = (f32[1,64,256]{1,2,0:T(8,128)}, f32[1,64,256]{1,2,0:T(8,128)}, u32[]{:S(2)}, u32[]{:S(2)}) collective-permute-start(f32[1,64,256]{1,2,0:T(8,128)} %get-tuple-element.402), channel_id=1, source_target_pairs={{1,0},{2,1},{3,2},{4,3},{5,4},{6,5},{7,6},{9,8},{10,9},{11,10},{12... | collective-permute-start | bytes 196616 | tf_op jit(solution)/shard_map/while/body/eval_jaxpr/ppermute | solution.py:22
  290.0 9.6 %collective-permute-start.1 = (f32[1,64,256]{1,2,0:T(8,128)}, f32[1,64,256]{1,2,0:T(8,128)}, u32[]{:S(2)}, u32[]{:S(2)}) collective-permute-start(f32[1,64,256]{1,2,0:T(8,128)} %get-tuple-element.403), channel_id=1, source_target_pairs={{0,1},{1,2},{2,3},{3,4},{4,5},{5,6},{6,7},{8,9},{9,10},{10,11},{11... | collective-permute-start | bytes 196616 | tf_op jit(solution)/shard_map/while/body/eval_jaxpr/ppermute | solution.py:20
  311.2 7.1 %collective-permute-start.2 = (f32[2,64,256]{2,1,0:T(8,128)S(1)}, f32[2,64,256]{2,1,0:T(8,128)}, u32[]{:S(2)}, u32[]{:S(2)}) collective-permute-start(f32[2,64,256]{2,1,0:T(8,128)S(1)} %bitcast.307), channel_id=1, source_target_pairs={{8,0},{16,8},{24,16},{9,1},{17,9},{25,17},{10,2},{18,10},{26,18},{... | collective-permute-start | bytes 393224 | tf_op jit(solution)/shard_map/while/body/eval_jaxpr/ppermute | solution.py:32
Sparse Core Ops, SparseCore 0:
  319.6 57.5 all-reduce.3
where the time goes:
time: 390 us; the launch traced here: 386 us
  matrix products  103 us (26%)
  waiting for transfers between devices  99.4 us (25%)
  local copies, waits for them, and re-layouts  92.1 us (24%)
  starting transfers between devices  54.4 us (14%)
  other arithmetic  21.6 us (6%)
  between operations  14.3 us (4%)
    dot_general x24, matrix products, apply_taps(): jnp.einsum('koc,dkcp->dop', kernel_taps[plane_shift], patches[plane_shift...  75.1 us
    psum x1, waiting for transfers between devices, per_device(): summed = lax.psum(filter_sum, 'depth')  57.7 us
    ppermute x7, waiting for transfers between devices, shifted(): return lax.ppermute(shard, axis, pairs)  41.7 us
    dot_general x21, matrix products, advance(): jnp.einsum('dop,dkcp->koc', own_slopes, patches[offset + plane_shift:offs...  27.8 us
    ppermute x8, starting transfers between devices, padded_2(): lax.ppermute(tail, axis, [(i, (i + 1) % count) for i in range(ends)])  25.3 us
    another operation x16, local copies, waits for them, and re-layouts, neighbours(): return jnp.stack(pieces, axis=1).reshape(planes, 9, channels, columns)  25 us
    ppermute x8, starting transfers between devices, padded_2(): lax.ppermute(head, axis, [((i + 1) % count, i) for i in range(ends)])  20.1 us
    slice x7, local copies, waits for them, and re-layouts, advance(): patches[offset + plane_shift:offset + plane_shift + slab_planes]  15.6 us
  transfers between devices with their start and end apart: 24, of which 8 were waited for; matrix products, arithmetic and copies ran while one was open for 15% of the time, Pallas kernels for 0%

commit v1 on v0

v1 whole, which is shorter than its diff:
```python
import functools
import math

import jax
import jax.numpy as jnp
from jax import lax
from jax.experimental import pallas as pl
from jax.experimental.pallas import tpu as pltpu
from jax.sharding import PartitionSpec as P

H = 16
W = 16
F32 = jnp.float32
BF16 = jnp.bfloat16
MESH = pl.DeviceIdType.MESH


def split(x):
    hi = x.astype(BF16)
    return hi, (x - hi.astype(F32)).astype(BF16)


def tap_masks(cells):
    lane = lax.broadcasted_iota(jnp.int32, (1, cells), 1)
    y, x = lane // W, lane % W
    masks = []
    for b in (-1, 0, 1):
        for c in (-1, 0, 1):
            masks.append((y + b >= 0) & (y + b < H) & (x + c >= 0) & (x + c < W))
    return masks


def put_patches(plane, hi_ref, lo_ref, masks):
    ch, cells = plane.shape
    for k in range(9):
        by = (k // 3 - 1) * W + (k % 3 - 1)
        v = plane if by == 0 else pltpu.roll(plane, (-by) % cells, 1)
        if by != 0:
            v = jnp.where(masks[k], v, 0.0)
        hi, lo = split(v)
        hi_ref[k * ch : (k + 1) * ch, :] = hi
        lo_ref[k * ch : (k + 1) * ch, :] = lo


def dot(a, b):
    return jnp.dot(a, b, preferred_element_type=F32)


def dot_nt(a, b):
    return lax.dot_general(a, b, (((1,), (1,)), ((), ())), preferred_element_type=F32)


def kernel(
    n_sec, n_dep, scale,
    act, filt, cot,
    grads, fsum,
    ext, fbuf, up, slope, gbuf, fsend, frecv,
    p_hi, p_lo, s_hi, s_lo, fs, fh, gs, gh, ss, sh, acc,
    own_sem, filt_sem, cot_sem, halo_send, halo_recv, face_send, face_recv, hop_send, hop_recv, out_sem,
):
    mb, sp, ch, cells = act.shape
    sec, dep = lax.axis_index("section"), lax.axis_index("depth")
    is_last = sec == n_sec - 1
    has_prev, has_next = dep > 0, dep < n_dep - 1
    masks = tap_masks(cells)

    def own_copy(m):
        return pltpu.make_async_copy(act.at[m], ext.at[m, pl.ds(1, sp)], own_sem.at[m])

    filt_copy = pltpu.make_async_copy(filt, fbuf, filt_sem)
    filt_copy.start()
    for m in range(mb):
        own_copy(m).start()

    @pl.when(is_last)
    def _():
        for m in range(mb):
            pltpu.make_async_copy(cot.at[m], up.at[m], cot_sem.at[m]).start()

    barrier = pltpu.get_barrier_semaphore()
    for target in (
        (sec, (dep + 1) % n_dep), (sec, (dep + n_dep - 1) % n_dep),
        ((sec + 1) % n_sec, dep), ((sec + n_sec - 1) % n_sec, dep),
    ):
        pl.semaphore_signal(barrier, inc=1, device_id=target, device_id_type=MESH)
    pl.semaphore_wait(barrier, 4)

    def halo_to_prev(m):
        return pltpu.make_async_remote_copy(
            act.at[m, 0], ext.at[m, sp + 1], halo_send.at[0, m], halo_recv.at[0, m],
            device_id=(sec, dep - 1), device_id_type=MESH)

    def halo_to_next(m):
        return pltpu.make_async_remote_copy(
            act.at[m, sp - 1], ext.at[m, 0], halo_send.at[1, m], halo_recv.at[1, m],
            device_id=(sec, dep + 1), device_id_type=MESH)

    def face_to_prev(m):
        return pltpu.make_async_remote_copy(
            fsend.at[m, 0], frecv.at[m, 1], face_send.at[0, m], face_recv.at[0, m],
            device_id=(sec, dep - 1), device_id_type=MESH)

    def face_to_next(m):
        return pltpu.make_async_remote_copy(
            fsend.at[m, 1], frecv.at[m, 0], face_send.at[1, m], face_recv.at[1, m],
            device_id=(sec, dep + 1), device_id_type=MESH)

    def hop(m):
        return pltpu.make_async_remote_copy(
            gbuf.at[m], up.at[m], hop_send.at[m], hop_recv.at[m],
            device_id=(sec - 1, dep), device_id_type=MESH)

    def out_copy(m):
        return pltpu.make_async_copy(gbuf.at[m], grads.at[m], out_sem.at[m])

    @pl.when(has_prev)
    def _():
        for m in range(mb):
            halo_to_prev(m).start()

    @pl.when(has_next)
    def _():
        for m in range(mb):
            halo_to_next(m).start()

    @pl.when(jnp.logical_not(has_prev))
    def _():
        for m in range(mb):
            ext[m, 0] = jnp.zeros((ch, cells), F32)
            frecv[m, 0] = jnp.zeros((ch, cells), F32)

    @pl.when(jnp.logical_not(has_next))
    def _():
        for m in range(mb):
            ext[m, sp + 1] = jnp.zeros((ch, cells), F32)
            frecv[m, 1] = jnp.zeros((ch, cells), F32)

    filt_copy.wait()
    for k in range(27):
        a, k9 = k // 9, k % 9
        w = fbuf[k]
        hi, lo = split(w)
        cols = slice(k9 * ch, (k9 + 1) * ch)
        fs[2 * a * ch : (2 * a + 1) * ch, cols] = hi
        fs[(2 * a + 1) * ch : (2 * a + 2) * ch, cols] = lo
        fh[a * ch : (a + 1) * ch, cols] = hi
        hi, lo = split(w.T)
        cols = slice((8 - k9) * ch, (9 - k9) * ch)
        gs[2 * a * ch : (2 * a + 1) * ch, cols] = hi
        gs[(2 * a + 1) * ch : (2 * a + 2) * ch, cols] = lo
        gh[a * ch : (a + 1) * ch, cols] = hi
    acc[...] = jnp.zeros_like(acc)

    def taps_of(e):
        return max(0, e - (sp - 1)), min(2, e)

    def prep(m):
        own_copy(m).wait()
        pre = [None] * sp
        for e in [*range(1, sp + 1), 0, sp + 1]:
            if e == 0:
                @pl.when(has_next)
                def _():
                    halo_to_prev(m).wait_recv()

                @pl.when(has_prev)
                def _():
                    halo_to_next(m).wait_recv()
            hi_ref, lo_ref = p_hi.at[m, e], p_lo.at[m, e]
            put_patches(ext[m, e], hi_ref, lo_ref, masks)
            a0, a1 = taps_of(e)
            yh = dot(fs[2 * a0 * ch : 2 * (a1 + 1) * ch, :], hi_ref[...])
            yl = dot(fh[a0 * ch : (a1 + 1) * ch, :], lo_ref[...])
            for a in range(a0, a1 + 1):
                j = a - a0
                part = (yh[2 * j * ch : (2 * j + 1) * ch] + yh[(2 * j + 1) * ch : (2 * j + 2) * ch]
                        + yl[j * ch : (j + 1) * ch])
                d = e - a
                pre[d] = part if pre[d] is None else pre[d] + part
        for d in range(sp):
            sg = jax.nn.sigmoid(pre[d])
            slope[m, d] = sg * (1.0 + pre[d] * (1.0 - sg))

    def back(d, a0, a1):
        yh = dot(gs[2 * a0 * ch : 2 * (a1 + 1) * ch, :], s_hi[d])
        yl = dot(gh[a0 * ch : (a1 + 1) * ch, :], s_lo[d])
        return [
            yh[2 * j * ch : (2 * j + 1) * ch] + yh[(2 * j + 1) * ch : (2 * j + 2) * ch] + yl[j * ch : (j + 1) * ch]
            for j in range(a1 - a0 + 1)
        ]

    prep(0)

    @pl.when(jnp.logical_not(is_last))
    def _():
        def more(m, carry):
            prep(m)
            return carry
        lax.fori_loop(1, mb, more, 0)

    def step(m, carry):
        @pl.when(is_last)
        def _():
            pltpu.make_async_copy(cot.at[m], up.at[m], cot_sem.at[m]).wait()

        @pl.when(jnp.logical_not(is_last))
        def _():
            hop(m).wait_recv()

        for d in range(sp):
            s = up[m, d] * slope[m, d]
            hi, lo = split(s)
            r = sp - 1 - d
            ss[2 * r * ch : (2 * r + 1) * ch, :] = hi
            ss[(2 * r + 1) * ch : (2 * r + 2) * ch, :] = lo
            sh[r * ch : (r + 1) * ch, :] = hi
            put_patches(s, s_hi.at[d], s_lo.at[d], masks)
        fsend[m, 0] = back(0, 0, 0)[0]

        @pl.when(has_prev)
        def _():
            face_to_prev(m).start()

        fsend[m, 1] = back(sp - 1, 2, 2)[0]

        @pl.when(has_next)
        def _():
            face_to_next(m).start()

        out = [None] * sp
        for d in range(sp):
            a0 = 1 if d == 0 else 0
            a1 = 1 if d == sp - 1 else 2
            for j, part in enumerate(back(d, a0, a1)):
                o = d + a0 + j - 1
                out[o] = part if out[o] is None else out[o] + part
        for d in range(sp):
            gbuf[m, d] = out[d]

        @pl.when(is_last & (m + 1 < mb))
        def _():
            prep(jnp.minimum(m + 1, mb - 1))

        @pl.when(has_next)
        def _():
            face_to_prev(m).wait_recv()

        @pl.when(has_prev)
        def _():
            face_to_next(m).wait_recv()

        gbuf[m, 0] = gbuf[m, 0] + frecv[m, 0]
        gbuf[m, sp - 1] = gbuf[m, sp - 1] + frecv[m, 1]

        @pl.when(sec > 0)
        def _():
            hop(m).start()

        out_copy(m).start()

        for e in range(sp + 2):
            a0, a1 = taps_of(e)
            r0 = sp - 1 - (e - a0)
            n = a1 - a0 + 1
            yh = dot_nt(ss[2 * r0 * ch : 2 * (r0 + n) * ch, :], p_hi[m, e])
            yl = dot_nt(sh[r0 * ch : (r0 + n) * ch, :], p_lo[m, e])
            for j in range(n):
                a = a0 + j
                acc[a * ch : (a + 1) * ch, :] += (
                    yh[2 * j * ch : (2 * j + 1) * ch] + yh[(2 * j + 1) * ch : (2 * j + 2) * ch]
                    + yl[j * ch : (j + 1) * ch])
        return carry

    lax.fori_loop(0, mb, step, 0)
    fsum[...] = acc[...] * scale

    for m in range(mb):
        out_copy(m).wait()

    @pl.when(has_prev)
    def _():
        for m in range(mb):
            halo_to_prev(m).wait_send()
            face_to_prev(m).wait_send()

    @pl.when(has_next)
    def _():
        for m in range(mb):
            halo_to_next(m).wait_send()
            face_to_next(m).wait_send()

    @pl.when(sec > 0)
    def _():
        for m in range(mb):
            hop(m).wait_send()


def per_device(n_sec, n_dep, activations, filters, cotangent):
    act, filt = activations[0], filters[0]
    mb, sp, ch, cells = act.shape
    scale = 1.0 / math.sqrt(mb * sp * n_dep * H * W)
    any_spec = pl.BlockSpec(memory_space=pl.ANY)
    dma = pltpu.SemaphoreType.DMA
    grads, fsum = pl.pallas_call(
        functools.partial(kernel, n_sec, n_dep, scale),
        out_shape=(
            jax.ShapeDtypeStruct(act.shape, F32),
            jax.ShapeDtypeStruct((3 * ch, 9 * ch), F32),
        ),
        in_specs=[any_spec] * 3,
        out_specs=(any_spec, pl.BlockSpec(memory_space=pltpu.VMEM)),
        scratch_shapes=[
            pltpu.VMEM((mb, sp + 2, ch, cells), F32),
            pltpu.VMEM(filt.shape, F32),
            pltpu.VMEM((mb, sp, ch, cells), F32),
            pltpu.VMEM((mb, sp, ch, cells), F32),
            pltpu.VMEM((mb, sp, ch, cells), F32),
            pltpu.VMEM((mb, 2, ch, cells), F32),
            pltpu.VMEM((mb, 2, ch, cells), F32),
            pltpu.VMEM((mb, sp + 2, 9 * ch, cells), BF16),
            pltpu.VMEM((mb, sp + 2, 9 * ch, cells), BF16),
            pltpu.VMEM((sp, 9 * ch, cells), BF16),
            pltpu.VMEM((sp, 9 * ch, cells), BF16),
            pltpu.VMEM((6 * ch, 9 * ch), BF16),
            pltpu.VMEM((3 * ch, 9 * ch), BF16),
            pltpu.VMEM((6 * ch, 9 * ch), BF16),
            pltpu.VMEM((3 * ch, 9 * ch), BF16),
            pltpu.VMEM((2 * sp * ch, cells), BF16),
            pltpu.VMEM((sp * ch, cells), BF16),
            pltpu.VMEM((3 * ch, 9 * ch), F32),
            dma((mb,)), dma, dma((mb,)),
            dma((2, mb)), dma((2, mb)), dma((2, mb)), dma((2, mb)),
            dma((mb,)), dma((mb,)), dma((mb,)),
        ],
        compiler_params=pltpu.CompilerParams(
            collective_id=0, has_side_effects=True, vmem_limit_bytes=48 * 1024 * 1024),
    )(act, filt, cotangent)
    summed = lax.psum(fsum, "depth")
    summed = summed.reshape(3, ch, 9, ch).transpose(0, 2, 1, 3).reshape(27, ch, ch)
    return grads[None], summed[None]


def solution(mesh):
    return jax.shard_map(
        functools.partial(per_device, mesh.shape["section"], mesh.shape["depth"]),
        mesh=mesh,
        in_specs=(
            P("section", None, "depth", None, None),
            P("section", None, None, None),
            P(None, "depth", None, None),
        ),
        out_specs=(P("section", None, "depth", None, None), P("section", None, None, None)),
        check_vma=False,
    )
```

time: 390 us -> 130 us (0.33)
  matrix products: 103 us -> 0 us
  local copies, waits for them, and re-layouts: 92.1 us -> 7.54 us
  starting transfers between devices: 54.4 us -> 0.04 us
  Pallas kernels: 0 us -> 53.1 us
  waiting for transfers between devices: 99.4 us -> 53.8 us
  other arithmetic: 21.6 us -> 0 us
    dot_general x45 -> x0, matrix products: 103 us -> none  [the longest x24 75.1 us: apply_taps(): jnp.einsum('koc,dkcp->dop', kernel_taps[plane_shift], patches[plane_shift...]
    ppermute x23 -> x0, starting transfers between devices: 54.3 us -> none  [the longest x8 25.3 us: padded_2(): lax.ppermute(tail, axis, [(i, (i + 1) % count) for i in range(ends)])]
    pallas_call x0 -> x1, Pallas kernels: none -> 53.1 us  [per_device(): pl.pallas_call(functools.partial(kernel, n_sec, n_dep, scale), out_shape=...]
    ppermute x23 -> x0, waiting for transfers between devices: 41.7 us -> none  [the longest x7 41.7 us: shifted(): return lax.ppermute(shard, axis, pairs)]
    slice x23 -> x0, local copies, waits for them, and re-layouts: 33.3 us -> none  [the longest x7 15.6 us: advance(): patches[offset + plane_shift:offset + plane_shift + slab_planes]]
    another operation x16 -> x0, local copies, waits for them, and re-layouts: 25 us -> none  [neighbours(): return jnp.stack(pieces, axis=1).reshape(planes, 9, channels, columns)]
    while x64 -> x0, local copies, waits for them, and re-layouts: 11.2 us -> none
    dynamic_slice x21 -> x0, local copies, waits for them, and re-layouts: 8.68 us -> none  [the longest x14 7.79 us: advance(): lax.dynamic_index_in_dim(slope_store, slot_index, 0, keepdims=False)]
  transfers between devices with their start and end apart: 24 -> 1, of which waited for: 8 -> 1; matrix products, arithmetic and copies ran while one was open for 15% -> 0% of each run, Pallas kernels for 0% -> 0%
where the time goes in v1:
time: 130 us; the launch traced here: 129 us
  waiting for transfers between devices  53.8 us (41%)
  Pallas kernels  53.1 us (41%)
  between operations  14.1 us (11%)
  local copies, waits for them, and re-layouts  7.54 us (6%)
    psum x1, waiting for transfers between devices, per_device(): summed = lax.psum(fsum, 'depth')  53.8 us
    pallas_call x1, Pallas kernels, per_device(): pl.pallas_call(functools.partial(kernel, n_sec, n_dep, scale), out_shape=...  53.1 us
    unnamed x10, local copies, waits for them, and re-layouts  5.51 us
  transfers between devices with their start and end apart: 1, of which 1 were waited for; matrix products, arithmetic and copies ran while one was open for 0% of the time, Pallas kernels for 0%

profile of v1, /device:TPU:1, one launch (start us, length us, event | category | flops | bytes accessed | tf_op | source)
XLA Modules:
  0.0 128.5 jit_solution(7757565535708799696)
XLA Ops:
  7.2 0.0 all-reduce.2.cloned.1.call-start
  7.2 0.0 copy-start
  7.2 1.2 copy-done
  8.4 0.0 copy-start.1
  8.4 1.0 copy-done.1
  9.4 0.0 copy-start.2
  9.4 1.0 copy-done.2
  10.5 53.1 %shard_map.50 = (f32[4,2,64,256]{3,2,1,0:T(8,128)S(1)}, f32[192,576]{1,0:T(8,128)S(1)}) custom-call(f32[4,2,64,256]{3,2,1,0:T(8,128)S(1)} %bitcast.9, f32[27,64,64]{2,1,0:T(8,128)S(1)} %bitcast.7, f32[4,2,64,256]{3,2,1,0:T(8,128)S(1)} %copy-done.2), custom_call_target="tpu_custom_call" | custom-call | tf_op jit(solution)/shard_map/pallas_call | solution.py:304
  63.6 0.2 copy.7
  63.8 0.4 reshape.7
  64.2 1.5 %copy.8 = f32[3,9,64,64]{3,2,1,0:T(8,128)} copy(f32[3,9,64,64]{2,0,3,1:T(4,128)S(1)} %bitcast.10) | data formatting | bytes 884736 | tf_op jit(solution)/shard_map/transpose | solution.py:339
  65.6 0.0 all-reduce.2.cloned.1.call-update
  65.6 53.8 %all-reduce.2.cloned.1.call-done = f32[1,27,64,64]{3,2,1,0:T(8,128)} async-done(((f32[1,27,64,64]{3,2,1,0:T(8,128)}), f32[1,27,64,64]{3,2,1,0:T(8,128)}) %all-reduce.2.cloned.1.call-update) | async-done | bytes 442384 | tf_op jit(solution)/shard_map/psum | solution.py:338
  119.4 0.0 copy-start.3
  119.4 0.8 copy.11
  120.2 0.6 copy-done.3
  120.8 0.9 copy.12
Async XLA Ops:
  7.2 112.3 %all-reduce.2.cloned.1.call-start = ((), (), s32[]{:S(2)}) async-start(), calls=%async_computation | async-start | bytes 1769472 | tf_op jit(solution)/shard_map/psum | solution.py:338
  7.2 1.2 copy-start
  8.4 1.0 copy-start.1
  9.4 1.0 copy-start.2
  119.4 1.4 %copy-start.3 = (f32[1,27,64,64]{3,2,1,0:T(8,128)S(1)}, f32[1,27,64,64]{3,2,1,0:T(8,128)}, u32[]{:S(2)}) copy-start(f32[1,27,64,64]{3,2,1,0:T(8,128)} %all-reduce.2.cloned.1.call-done) | copy-start | bytes 1327108
Sparse Core Ops, SparseCore 0:
  65.8 53.6 all-reduce.1

commit v2 on v1

--- a/solution.py
+++ b/solution.py
@@ -56,7 +56,9 @@
     grads, fsum,
     ext, fbuf, up, slope, gbuf, fsend, frecv,
     p_hi, p_lo, s_hi, s_lo, fs, fh, gs, gh, ss, sh, acc,
+    pbuf, hbuf, cbuf, full,
     own_sem, filt_sem, cot_sem, halo_send, halo_recv, face_send, face_recv, hop_send, hop_recv, out_sem,
+    pair_send, pair_recv, rs_send, rs_recv, ag_send, ag_recv, fw_send, fw_recv, fout_sem,
 ):
     mb, sp, ch, cells = act.shape
     sec, dep = lax.axis_index("section"), lax.axis_index("depth")
@@ -77,13 +79,24 @@
         for m in range(mb):
             pltpu.make_async_copy(cot.at[m], up.at[m], cot_sem.at[m]).start()
 
+    n2 = n_dep // 2
+    half = acc.shape[0] // 2
+    rs = half // n2
+    zed, core = dep // 2, dep % 2
+    partner = (sec, zed * 2 + 1 - core)
+
+    def peer(t):
+        return (sec, ((zed + t) % n2) * 2 + core)
+
     barrier = pltpu.get_barrier_semaphore()
+    for t in range(1, n2):
+        pl.semaphore_signal(barrier, inc=1, device_id=peer(t), device_id_type=MESH)
     for target in (
         (sec, (dep + 1) % n_dep), (sec, (dep + n_dep - 1) % n_dep),
         ((sec + 1) % n_sec, dep), ((sec + n_sec - 1) % n_sec, dep),
     ):
         pl.semaphore_signal(barrier, inc=1, device_id=target, device_id_type=MESH)
-    pl.semaphore_wait(barrier, 4)
+    pl.semaphore_wait(barrier, 3 + n2)
 
     def halo_to_prev(m):
         return pltpu.make_async_remote_copy(
@@ -112,6 +125,29 @@
 
     def out_copy(m):
         return pltpu.make_async_copy(gbuf.at[m], grads.at[m], out_sem.at[m])
+
+    def remote(src, dst, send, recv, target):
+        return pltpu.make_async_remote_copy(src, dst, send, recv, device_id=target, device_id_type=MESH)
+
+    def pair():
+        theirs = pl.multiple_of((1 - core) * half, 8)
+        return remote(acc.at[pl.ds(theirs, half)], pbuf, pair_send, pair_recv, partner)
+
+    def scatter(t):
+        rows = pl.ds(pl.multiple_of(((zed + t) % n2) * rs, 8), rs)
+        return remote(hbuf.at[rows], cbuf.at[t - 1], rs_send.at[t - 1], rs_recv.at[t - 1], peer(t))
+
+    def rows_of(t):
+        return pl.ds(pl.multiple_of(core * half + ((zed + n2 - t) % n2) * rs, 8), rs)
+
+    def gather(t):
+        return remote(full.at[rows_of(0)], full.at[rows_of(0)], ag_send.at[t - 1], ag_recv.at[t - 1], peer(t))
+
+    def arrived(t):
+        return remote(full.at[rows_of(t)], full.at[rows_of(t)], ag_send.at[t - 1], ag_recv.at[t - 1], peer(t))
+
+    def forward(t):
+        return remote(full.at[rows_of(t)], full.at[rows_of(t)], fw_send.at[t], fw_recv.at[t], partner)
 
     @pl.when(has_prev)
     def _():
@@ -189,75 +225,7 @@
             for j in range(a1 - a0 + 1)
         ]
 
-    prep(0)
-
-    @pl.when(jnp.logical_not(is_last))
-    def _():
-        def more(m, carry):
-            prep(m)
-            return carry
-        lax.fori_loop(1, mb, more, 0)
-
-    def step(m, carry):
-        @pl.when(is_last)
-        def _():
-            pltpu.make_async_copy(cot.at[m], up.at[m], cot_sem.at[m]).wait()
-
-        @pl.when(jnp.logical_not(is_last))
-        def _():
-            hop(m).wait_recv()
-
-        for d in range(sp):
-            s = up[m, d] * slope[m, d]
-            hi, lo = split(s)
-            r = sp - 1 - d
-            ss[2 * r * ch : (2 * r + 1) * ch, :] = hi
-            ss[(2 * r + 1) * ch : (2 * r + 2) * ch, :] = lo
-            sh[r * ch : (r + 1) * ch, :] = hi
-            put_patches(s, s_hi.at[d], s_lo.at[d], masks)
-        fsend[m, 0] = back(0, 0, 0)[0]
-
-        @pl.when(has_prev)
-        def _():
-            face_to_prev(m).start()
-
-        fsend[m, 1] = back(sp - 1, 2, 2)[0]
-
-        @pl.when(has_next)
-        def _():
-            face_to_next(m).start()
-
-        out = [None] * sp
-        for d in range(sp):
-            a0 = 1 if d == 0 else 0
-            a1 = 1 if d == sp - 1 else 2
-            for j, part in enumerate(back(d, a0, a1)):
-                o = d + a0 + j - 1
-                out[o] = part if out[o] is None else out[o] + part
-        for d in range(sp):
-            gbuf[m, d] = out[d]
-
-        @pl.when(is_last & (m + 1 < mb))
-        def _():
-            prep(jnp.minimum(m + 1, mb - 1))
-
-        @pl.when(has_next)
-        def _():
-            face_to_prev(m).wait_recv()
-
-        @pl.when(has_prev)
-        def _():
-            face_to_next(m).wait_recv()
-
-        gbuf[m, 0] = gbuf[m, 0] + frecv[m, 0]
-        gbuf[m, sp - 1] = gbuf[m, sp - 1] + frecv[m, 1]
-
-        @pl.when(sec > 0)
-        def _():
-            hop(m).start()
-
-        out_copy(m).start()
-
+    def filter_terms(m):
         for e in range(sp + 2):
             a0, a1 = taps_of(e)
             r0 = sp - 1 - (e - a0)
@@ -269,10 +237,130 @@
                 acc[a * ch : (a + 1) * ch, :] += (
                     yh[2 * j * ch : (2 * j + 1) * ch] + yh[(2 * j + 1) * ch : (2 * j + 2) * ch]
                     + yl[j * ch : (j + 1) * ch])
+
+    prep(0)
+
+    @pl.when(jnp.logical_not(is_last))
+    def _():
+        def more(m, carry):
+            prep(m)
+            return carry
+        lax.fori_loop(1, mb, more, 0)
+
+    def step(m, carry):
+        @pl.when(is_last)
+        def _():
+            pltpu.make_async_copy(cot.at[m], up.at[m], cot_sem.at[m]).wait()
+
+        @pl.when(jnp.logical_not(is_last))
+        def _():
+            hop(m).wait_recv()
+
+        def cotangents(d):
+            s = up[m, d] * slope[m, d]
+            hi, lo = split(s)
+            r = sp - 1 - d
+            ss[2 * r * ch : (2 * r + 1) * ch, :] = hi
+            ss[(2 * r + 1) * ch : (2 * r + 2) * ch, :] = lo
+            sh[r * ch : (r + 1) * ch, :] = hi
+            put_patches(s, s_hi.at[d], s_lo.at[d], masks)
+
+        cotangents(0)
+        fsend[m, 0] = back(0, 0, 0)[0]
+
+        @pl.when(has_prev)
+        def _():
+            face_to_prev(m).start()
+
+        for d in range(1, sp):
+            cotangents(d)
+        fsend[m, 1] = back(sp - 1, 2, 2)[0]
+
+        @pl.when(has_next)
+        def _():
+            face_to_next(m).start()
+
+        @pl.when(sec == 0)
+        def _():
+            filter_terms(m)
+
+        @pl.when((sec == 0) & (m == mb - 1))
+        def _():
+            pair().start()
+
+        out = [None] * sp
+        for d in range(sp):
+            a0 = 1 if d == 0 else 0
+            a1 = 1 if d == sp - 1 else 2
+            for j, part in enumerate(back(d, a0, a1)):
+                o = d + a0 + j - 1
+                out[o] = part if out[o] is None else out[o] + part
+        for d in range(sp):
+            gbuf[m, d] = out[d]
+
+        @pl.when(is_last & (m + 1 < mb))
+        def _():
+            prep(jnp.minimum(m + 1, mb - 1))
+
+        @pl.when(has_next)
+        def _():
+            face_to_prev(m).wait_recv()
+
+        @pl.when(has_prev)
+        def _():
+            face_to_next(m).wait_recv()
+
+        gbuf[m, 0] = gbuf[m, 0] + frecv[m, 0]
+        gbuf[m, sp - 1] = gbuf[m, sp - 1] + frecv[m, 1]
+
+        @pl.when(sec > 0)
+        def _():
+            hop(m).start()
+
+        out_copy(m).start()
+
+        @pl.when(sec > 0)
+        def _():
+            filter_terms(m)
+
         return carry
 
     lax.fori_loop(0, mb, step, 0)
-    fsum[...] = acc[...] * scale
+
+    @pl.when(sec > 0)
+    def _():
+        pair().start()
+
+    mine = pl.multiple_of(core * half, 8)
+    pair().wait_recv()
+    hbuf[...] = acc[pl.ds(mine, half), :] + pbuf[...]
+    for t in range(1, n2):
+        scatter(t).start()
+    total = hbuf[pl.ds(pl.multiple_of(zed * rs, 8), rs), :]
+    for t in range(1, n2):
+        scatter(t).wait_recv()
+        total = total + cbuf[t - 1]
+    full[rows_of(0), :] = total * scale
+    for t in range(1, n2):
+        gather(t).start()
+    forward(0).start()
+    for t in range(1, n2):
+        arrived(t).wait_recv()
+        forward(t).start()
+    for t in range(n2):
+        forward(t).wait_recv()
+    for k in range(27):
+        a, k9 = k // 9, k % 9
+        fbuf[k] = full[a * ch : (a + 1) * ch, k9 * ch : (k9 + 1) * ch]
+    fout = pltpu.make_async_copy(fbuf, fsum, fout_sem)
+    fout.start()
+    pair().wait_send()
+    for t in range(1, n2):
+        scatter(t).wait_send()
+        gather(t).wait_send()
+    for t in range(n2):
+        forward(t).wait_send()
+    fout.wait()
 
     for m in range(mb):
         out_copy(m).wait()
@@ -300,15 +388,18 @@
     mb, sp, ch, cells = act.shape
     scale = 1.0 / math.sqrt(mb * sp * n_dep * H * W)
     any_spec = pl.BlockSpec(memory_space=pl.ANY)
+    hbm_spec = pl.BlockSpec(memory_space=pltpu.MemorySpace.HBM)
+    n2 = n_dep // 2
+    rs = 8 * pl.cdiv(3 * ch, 16 * n2)
     dma = pltpu.SemaphoreType.DMA
     grads, fsum = pl.pallas_call(
         functools.partial(kernel, n_sec, n_dep, scale),
         out_shape=(
             jax.ShapeDtypeStruct(act.shape, F32),
-            jax.ShapeDtypeStruct((3 * ch, 9 * ch), F32),
+            jax.ShapeDtypeStruct(filt.shape, F32),
         ),
-        in_specs=[any_spec] * 3,
-        out_specs=(any_spec, pl.BlockSpec(memory_space=pltpu.VMEM)),
+        in_specs=[hbm_spec] * 3,
+        out_specs=(any_spec, any_spec),
         scratch_shapes=[
             pltpu.VMEM((mb, sp + 2, ch, cells), F32),
             pltpu.VMEM(filt.shape, F32),
@@ -327,17 +418,20 @@
             pltpu.VMEM((3 * ch, 9 * ch), BF16),
             pltpu.VMEM((2 * sp * ch, cells), BF16),
             pltpu.VMEM((sp * ch, cells), BF16),
-            pltpu.VMEM((3 * ch, 9 * ch), F32),
+            pltpu.VMEM((2 * n2 * rs, 9 * ch), F32),
+            pltpu.VMEM((n2 * rs, 9 * ch), F32),
+            pltpu.VMEM((n2 * rs, 9 * ch), F32),
+            pltpu.VMEM((max(n2 - 1, 1), rs, 9 * ch), F32),
+            pltpu.VMEM((2 * n2 * rs, 9 * ch), F32),
             dma((mb,)), dma, dma((mb,)),
             dma((2, mb)), dma((2, mb)), dma((2, mb)), dma((2, mb)),
             dma((mb,)), dma((mb,)), dma((mb,)),
+            dma, dma, dma((n2,)), dma((n2,)), dma((n2,)), dma((n2,)), dma((n2,)), dma((n2,)), dma,
         ],
         compiler_params=pltpu.CompilerParams(
             collective_id=0, has_side_effects=True, vmem_limit_bytes=48 * 1024 * 1024),
     )(act, filt, cotangent)
-    summed = lax.psum(fsum, "depth")
-    summed = summed.reshape(3, ch, 9, ch).transpose(0, 2, 1, 3).reshape(27, ch, ch)
-    return grads[None], summed[None]
+    return grads[None], fsum[None]
 
 
 def solution(mesh):

time: 130 us -> 73.1 us (0.56)
  waiting for transfers between devices: 53.8 us -> 0 us
  Pallas kernels: 53.1 us -> 67.3 us
  between operations: 14.1 us -> 0.65 us
  local copies, waits for them, and re-layouts: 7.54 us -> 4.95 us
    psum x1 -> x0, waiting for transfers between devices: 53.8 us -> none  [per_device(): summed = lax.psum(fsum, 'depth')]
    pallas_call x1, Pallas kernels: 53.1 us -> 67.3 us  [per_device(): pl.pallas_call(functools.partial(kernel, n_sec, n_dep, scale), out_shape=...]
    transpose x1 -> x0, local copies, waits for them, and re-layouts: 1.46 us -> none  [per_device(): summed.reshape(3, ch, 9, ch).transpose(0, 2, 1, 3).reshape(27, ch, ch)]
    unnamed x10 -> x8, local copies, waits for them, and re-layouts: 5.51 us -> 4.95 us
  transfers between devices with their start and end apart: 1 -> 0, of which waited for: 1 -> 0; matrix products, arithmetic and copies ran while one was open for 0% -> 0% of each run, Pallas kernels for 0% -> 0%
where the time goes in v2:
time: 73.1 us; the launch traced here: 72.9 us
  Pallas kernels  67.3 us (92%)
  local copies, waits for them, and re-layouts  4.95 us (7%)
    pallas_call x1, Pallas kernels, per_device(): pl.pallas_call(functools.partial(kernel, n_sec, n_dep, scale), out_shape=...  67.3 us
    unnamed x8, local copies, waits for them, and re-layouts  4.95 us

profile of v2, /device:TPU:1, one launch (start us, length us, event | category | flops | bytes accessed | tf_op | source)
XLA Modules:
  0.0 72.9 jit_solution(17681082979292572353)
XLA Ops:
  0.6 0.0 copy-start
  0.6 1.2 %copy-done = f32[1,27,64,64]{3,2,1,0:T(8,128)S(1)} copy-done((f32[1,27,64,64]{3,2,1,0:T(8,128)S(1)}, f32[1,27,64,64]{3,2,1,0:T(8,128)}, u32[]{:S(2)}) %copy-start) | copy-done | bytes 442392
  1.8 0.0 copy-start.1
  1.8 1.0 %copy-done.1 = f32[1,4,2,64,256]{4,3,2,1,0:T(8,128)S(1)} copy-done((f32[1,4,2,64,256]{4,3,2,1,0:T(8,128)S(1)}, f32[1,4,2,64,256]{4,3,2,1,0:T(8,128)}, u32[]{:S(2)}) %copy-start.1) | copy-done | bytes 524312
  2.8 0.0 copy-start.2
  2.8 1.0 %copy-done.2 = f32[4,2,64,256]{3,2,1,0:T(8,128)S(1)} copy-done((f32[4,2,64,256]{3,2,1,0:T(8,128)S(1)}, f32[4,2,64,256]{3,2,1,0:T(8,128)}, u32[]{:S(2)}) %copy-start.2) | copy-done | bytes 524312
  3.9 67.3 %shard_map.50 = (f32[4,2,64,256]{3,2,1,0:T(8,128)S(1)}, f32[27,64,64]{2,1,0:T(8,128)S(1)}) custom-call(f32[4,2,64,256]{3,2,1,0:T(8,128)S(1)} %bitcast.7, f32[27,64,64]{2,1,0:T(8,128)S(1)} %bitcast.5, f32[4,2,64,256]{3,2,1,0:T(8,128)S(1)} %copy-done.2), custom_call_target="tpu_custom_call" | custom-call | tf_op jit(solution)/shard_map/pallas_call | solution.py:395
  71.2 0.8 %copy.7 = f32[1,4,2,64,256]{4,3,2,1,0:T(8,128)} copy(f32[1,4,2,64,256]{4,3,2,1,0:T(8,128)S(1)} %bitcast.6) | data formatting | bytes 1048576
  72.0 0.9 %copy.8 = f32[1,27,64,64]{3,2,1,0:T(8,128)} copy(f32[1,27,64,64]{3,2,1,0:T(8,128)S(1)} %bitcast.4) | data formatting | bytes 884736
Async XLA Ops:
  0.6 1.2 %copy-start = (f32[1,27,64,64]{3,2,1,0:T(8,128)S(1)}, f32[1,27,64,64]{3,2,1,0:T(8,128)}, u32[]{:S(2)}) copy-start(f32[1,27,64,64]{3,2,1,0:T(8,128)} %param.4) | copy-start | bytes 1327108
  1.8 1.0 %copy-start.1 = (f32[1,4,2,64,256]{4,3,2,1,0:T(8,128)S(1)}, f32[1,4,2,64,256]{4,3,2,1,0:T(8,128)}, u32[]{:S(2)}) copy-start(f32[1,4,2,64,256]{4,3,2,1,0:T(8,128)} %param.3) | copy-start | bytes 1572868
  2.8 1.0 %copy-start.2 = (f32[4,2,64,256]{3,2,1,0:T(8,128)S(1)}, f32[4,2,64,256]{3,2,1,0:T(8,128)}, u32[]{:S(2)}) copy-start(f32[4,2,64,256]{3,2,1,0:T(8,128)} %cot.1) | copy-start | bytes 1572868

commit v3 on v2

v3 whole, which is shorter than its diff:
```python
import functools
import math

import jax
import jax.numpy as jnp
from jax import lax
from jax.experimental import pallas as pl
from jax.experimental.pallas import tpu as pltpu
from jax.sharding import PartitionSpec as P

H = 16
W = 16
F32 = jnp.float32
BF16 = jnp.bfloat16
MESH = pl.DeviceIdType.MESH


def split(x):
    hi = x.astype(BF16)
    return hi, (x - hi.astype(F32)).astype(BF16)


def tap_masks(cells):
    lane = lax.broadcasted_iota(jnp.int32, (1, cells), 1)
    y, x = lane // W, lane % W
    masks = []
    for b in (-1, 0, 1):
        for c in (-1, 0, 1):
            masks.append((y + b >= 0) & (y + b < H) & (x + c >= 0) & (x + c < W))
    return masks


def put_patches(plane, hi_ref, lo_ref, masks):
    ch, cells = plane.shape
    for k in range(9):
        by = (k // 3 - 1) * W + (k % 3 - 1)
        v = plane if by == 0 else pltpu.roll(plane, (-by) % cells, 1)
        if by != 0:
            v = jnp.where(masks[k], v, 0.0)
        hi, lo = split(v)
        hi_ref[k * ch : (k + 1) * ch, :] = hi
        lo_ref[k * ch : (k + 1) * ch, :] = lo


def dot(a, b):
    return jnp.dot(a, b, preferred_element_type=F32)


def dot_nt(a, b):
    return lax.dot_general(a, b, (((1,), (1,)), ((), ())), preferred_element_type=F32)


def kernel(
    n_sec, n_dep, scale,
    act, filt, cot,
    grads, fsum,
    ext, fbuf, up, slope, gbuf, fsend, frecv,
    p_hi, p_lo, s_hi, s_lo, fs, fh, gs, gh, ss, sh, acc,
    pbuf, hbuf, cbuf, full,
    own_sem, filt_sem, cot_sem, halo_send, halo_recv, face_send, face_recv, hop_send, hop_recv, out_sem,
    pair_send, pair_recv, rs_send, rs_recv, ag_send, ag_recv, fw_send, fw_recv, fout_sem,
):
    mb, sp, ch, cells = act.shape
    sec, dep = lax.axis_index("section"), lax.axis_index("depth")
    n2 = n_dep // 2
    zed, core = dep // 2, dep % 2
    is_last = sec == n_sec - 1
    toward = 2 * core - 1
    outer_dep = dep + toward
    has_outer = (outer_dep >= 0) & (outer_dep < n_dep)
    partner, outside = (sec, dep - toward), (sec, outer_dep)
    masks = tap_masks(cells)

    def plane(j):
        return core * j + (1 - core) * (sp - 1 - j)

    def tap(a):
        return core * a + (1 - core) * (2 - a)

    def remote(src, dst, send, recv, target):
        return pltpu.make_async_remote_copy(src, dst, send, recv, device_id=target, device_id_type=MESH)

    def own_copy(m, j):
        return pltpu.make_async_copy(act.at[m, plane(j)], ext.at[m, j + 1], own_sem.at[m, j])

    def cot_copy(m, j):
        return pltpu.make_async_copy(cot.at[m, plane(j)], up.at[m, j], cot_sem.at[m, j])

    filt_copy = pltpu.make_async_copy(filt, fbuf, filt_sem)
    filt_copy.start()
    for m in range(mb):
        for j in range(sp):
            own_copy(m, j).start()

    @pl.when(is_last)
    def _():
        for m in range(mb):
            for j in range(sp):
                cot_copy(m, j).start()

    half = acc.shape[0] // 2
    rs = half // n2
    pieces = rs // 8

    def peer(t):
        return (sec, ((zed + t) % n2) * 2 + core)

    barrier = pltpu.get_barrier_semaphore()
    for target in (
        (sec, (dep + 1) % n_dep), (sec, (dep + n_dep - 1) % n_dep),
        ((sec + 1) % n_sec, dep), ((sec + n_sec - 1) % n_sec, dep),
        *(peer(t) for t in range(1, n2)),
    ):
        pl.semaphore_signal(barrier, inc=1, device_id=target, device_id_type=MESH)
    pl.semaphore_wait(barrier, 3 + n2)

    def halo_in(m):
        return remote(act.at[m, plane(0)], ext.at[m, 0], halo_send.at[0, m], halo_recv.at[0, m], partner)

    def halo_out(m):
        return remote(act.at[m, plane(sp - 1)], ext.at[m, sp + 1], halo_send.at[1, m], halo_recv.at[1, m], outside)

    def face_in(m):
        return remote(fsend.at[m, 0], frecv.at[m, 0], face_send.at[0, m], face_recv.at[0, m], partner)

    def face_out(m):
        return remote(fsend.at[m, 1], frecv.at[m, 1], face_send.at[1, m], face_recv.at[1, m], outside)

    def hop(m, j):
        return remote(gbuf.at[m, j], up.at[m, j], hop_send.at[m, j], hop_recv.at[m, j], (sec - 1, dep))

    def out_copy(m, j):
        return pltpu.make_async_copy(gbuf.at[m, j], grads.at[m, plane(j)], out_sem.at[m, j])

    def pair():
        theirs = pl.multiple_of((1 - core) * half, 8)
        return remote(acc.at[pl.ds(theirs, half)], pbuf, pair_send, pair_recv, partner)

    def scatter(p, t):
        rows = pl.ds(pl.multiple_of(((zed + t) % n2) * rs + p * 8, 8), 8)
        return remote(hbuf.at[rows], cbuf.at[t - 1, pl.ds(p * 8, 8)], rs_send.at[p, t - 1], rs_recv.at[p, t - 1], peer(t))

    def rows_of(p, t):
        return pl.ds(pl.multiple_of(core * half + ((zed + n2 - t) % n2) * rs + p * 8, 8), 8)

    def gather(p, t):
        rows = rows_of(p, 0)
        return remote(full.at[rows], full.at[rows], ag_send.at[p, t - 1], ag_recv.at[p, t - 1], peer(t))

    def arrived(p, t):
        rows = rows_of(p, t)
        return remote(full.at[rows], full.at[rows], ag_send.at[p, t - 1], ag_recv.at[p, t - 1], peer(t))

    def forward(p, t):
        rows = rows_of(p, t)
        return remote(full.at[rows], full.at[rows], fw_send.at[p, t], fw_recv.at[p, t], partner)

    for m in range(mb):
        halo_in(m).start()

    @pl.when(has_outer)
    def _():
        for m in range(mb):
            halo_out(m).start()

    @pl.when(jnp.logical_not(has_outer))
    def _():
        for m in range(mb):
            ext[m, sp + 1] = jnp.zeros((ch, cells), F32)
            frecv[m, 1] = jnp.zeros((ch, cells), F32)

    filt_copy.wait()
    for a in range(3):
        r = tap(a)
        two, one = pl.multiple_of(2 * r * ch, 2 * ch), pl.multiple_of(r * ch, ch)
        for k9 in range(9):
            w = fbuf[9 * a + k9]
            hi, lo = split(w)
            cols = slice(k9 * ch, (k9 + 1) * ch)
            fs[pl.ds(two, ch), cols] = hi
            fs[pl.ds(two + ch, ch), cols] = lo
            fh[pl.ds(one, ch), cols] = hi
            hi, lo = split(w.T)
            cols = slice((8 - k9) * ch, (9 - k9) * ch)
            gs[pl.ds(two, ch), cols] = hi
            gs[pl.ds(two + ch, ch), cols] = lo
            gh[pl.ds(one, ch), cols] = hi
    acc[...] = jnp.zeros_like(acc)

    def taps_of(e):
        return max(0, e - (sp - 1)), min(2, e)

    def parts(yh, yl, n):
        return [
            yh[2 * i * ch : (2 * i + 1) * ch] + yh[(2 * i + 1) * ch : (2 * i + 2) * ch] + yl[i * ch : (i + 1) * ch]
            for i in range(n)
        ]

    def prep(m):
        pre = [None] * sp
        for e in [*range(1, sp + 1), 0, sp + 1]:
            if e == 0:
                halo_in(m).wait_recv()
            elif e <= sp:
                own_copy(m, e - 1).wait()
            else:
                @pl.when(has_outer)
                def _():
                    halo_out(m).wait_recv()
            hi_ref, lo_ref = p_hi.at[m, e], p_lo.at[m, e]
            put_patches(ext[m, e], hi_ref, lo_ref, masks)
            a0, a1 = taps_of(e)
            yh = dot(fs[2 * a0 * ch : 2 * (a1 + 1) * ch, :], hi_ref[...])
            yl = dot(fh[a0 * ch : (a1 + 1) * ch, :], lo_ref[...])
            for i, part in enumerate(parts(yh, yl, a1 - a0 + 1)):
                d = e - a0 - i
                pre[d] = part if pre[d] is None else pre[d] + part
        for d in range(sp):
            sg = jax.nn.sigmoid(pre[d])
            slope[m, d] = sg * (1.0 + pre[d] * (1.0 - sg))

    def back(d, a0, a1):
        yh = dot(gs[2 * a0 * ch : 2 * (a1 + 1) * ch, :], s_hi[d])
        yl = dot(gh[a0 * ch : (a1 + 1) * ch, :], s_lo[d])
        return parts(yh, yl, a1 - a0 + 1)

    def filter_terms(m):
        for e in range(sp + 2):
            a0, a1 = taps_of(e)
            r0 = sp - 1 - (e - a0)
            n = a1 - a0 + 1
            yh = dot_nt(ss[2 * r0 * ch : 2 * (r0 + n) * ch, :], p_hi[m, e])
            yl = dot_nt(sh[r0 * ch : (r0 + n) * ch, :], p_lo[m, e])
            for i, part in enumerate(parts(yh, yl, n)):
                rows = pl.ds(pl.multiple_of(tap(a0 + i) * ch, ch), ch)
                acc[rows, :] += part

    prep(0)

    @pl.when(jnp.logical_not(is_last))
    def _():
        def more(m, carry):
            prep(m)
            return carry
        lax.fori_loop(1, mb, more, 0)

    def step(m, carry):
        def cotangents(d):
            @pl.when(is_last)
            def _():
                cot_copy(m, d).wait()

            @pl.when(jnp.logical_not(is_last))
            def _():
                hop(m, d).wait_recv()

            s = up[m, d] * slope[m, d]
            hi, lo = split(s)
            r = sp - 1 - d
            ss[2 * r * ch : (2 * r + 1) * ch, :] = hi
            ss[(2 * r + 1) * ch : (2 * r + 2) * ch, :] = lo
            sh[r * ch : (r + 1) * ch, :] = hi
            put_patches(s, s_hi.at[d], s_lo.at[d], masks)

        def leave(j):
            @pl.when(sec > 0)
            def _():
                hop(m, j).start()

            out_copy(m, j).start()

        cotangents(0)
        fsend[m, 0] = back(0, 0, 0)[0]
        face_in(m).start()
        for d in range(1, sp):
            cotangents(d)
        fsend[m, 1] = back(sp - 1, 2, 2)[0]

        @pl.when(has_outer)
        def _():
            face_out(m).start()

        @pl.when(sec == 0)
        def _():
            filter_terms(m)

        @pl.when((sec == 0) & (m == mb - 1))
        def _():
            pair().start()

        out = [None] * sp
        for d in range(sp):
            a0 = 1 if d == 0 else 0
            a1 = 1 if d == sp - 1 else 2
            for i, part in enumerate(back(d, a0, a1)):
                o = d + a0 + i - 1
                out[o] = part if out[o] is None else out[o] + part
        for d in range(1, sp):
            gbuf[m, d] = out[d]
        face_in(m).wait_recv()
        gbuf[m, 0] = out[0] + frecv[m, 0]
        for j in range(sp - 1):
            leave(j)

        @pl.when(sec > 0)
        def _():
            filter_terms(m)

        @pl.when(is_last & (m + 1 < mb))
        def _():
            prep(jnp.minimum(m + 1, mb - 1))

        @pl.when(has_outer)
        def _():
            face_out(m).wait_recv()

        gbuf[m, sp - 1] = gbuf[m, sp - 1] + frecv[m, 1]
        leave(sp - 1)
        return carry

    lax.fori_loop(0, mb, step, 0)

    @pl.when(sec > 0)
    def _():
        pair().start()

    mine = pl.multiple_of(core * half, 8)
    pair().wait_recv()
    hbuf[...] = acc[pl.ds(mine, half), :] + pbuf[...]
    for p in range(pieces):
        for t in range(1, n2):
            scatter(p, t).start()
    for p in range(pieces):
        total = hbuf[pl.ds(pl.multiple_of(zed * rs + p * 8, 8), 8), :]
        for t in range(1, n2):
            scatter(p, t).wait_recv()
            total = total + cbuf[t - 1, p * 8 : (p + 1) * 8, :]
        full[rows_of(p, 0), :] = total * scale
        for t in range(1, n2):
            gather(p, t).start()
        forward(p, 0).start()
    for p in range(pieces):
        for t in range(1, n2):
            arrived(p, t).wait_recv()
            forward(p, t).start()
    for p in range(pieces):
        for t in range(n2):
            forward(p, t).wait_recv()
    for k in range(27):
        a, k9 = k // 9, k % 9
        fbuf[k] = full[a * ch : (a + 1) * ch, k9 * ch : (k9 + 1) * ch]
    fout = pltpu.make_async_copy(fbuf, fsum, fout_sem)
    fout.start()
    pair().wait_send()
    for p in range(pieces):
        for t in range(1, n2):
            scatter(p, t).wait_send()
            gather(p, t).wait_send()
        for t in range(n2):
            forward(p, t).wait_send()
    for m in range(mb):
        halo_in(m).wait_send()
        face_in(m).wait_send()
        for j in range(sp):
            out_copy(m, j).wait()

    @pl.when(has_outer)
    def _():
        for m in range(mb):
            halo_out(m).wait_send()
            face_out(m).wait_send()

    @pl.when(sec > 0)
    def _():
        for m in range(mb):
            for j in range(sp):
                hop(m, j).wait_send()

    fout.wait()


def per_device(n_sec, n_dep, activations, filters, cotangent):
    act, filt = activations[0], filters[0]
    mb, sp, ch, cells = act.shape
    scale = 1.0 / math.sqrt(mb * sp * n_dep * H * W)
    any_spec = pl.BlockSpec(memory_space=pl.ANY)
    hbm_spec = pl.BlockSpec(memory_space=pltpu.MemorySpace.HBM)
    n2 = n_dep // 2
    rs = 8 * pl.cdiv(3 * ch, 16 * n2)
    dma = pltpu.SemaphoreType.DMA
    grads, fsum = pl.pallas_call(
        functools.partial(kernel, n_sec, n_dep, scale),
        out_shape=(
            jax.ShapeDtypeStruct(act.shape, F32),
            jax.ShapeDtypeStruct(filt.shape, F32),
        ),
        in_specs=[hbm_spec] * 3,
        out_specs=(any_spec, any_spec),
        scratch_shapes=[
            pltpu.VMEM((mb, sp + 2, ch, cells), F32),
            pltpu.VMEM(filt.shape, F32),
            pltpu.VMEM((mb, sp, ch, cells), F32),
            pltpu.VMEM((mb, sp, ch, cells), F32),
            pltpu.VMEM((mb, sp, ch, cells), F32),
            pltpu.VMEM((mb, 2, ch, cells), F32),
            pltpu.VMEM((mb, 2, ch, cells), F32),
            pltpu.VMEM((mb, sp + 2, 9 * ch, cells), BF16),
            pltpu.VMEM((mb, sp + 2, 9 * ch, cells), BF16),
            pltpu.VMEM((sp, 9 * ch, cells), BF16),
            pltpu.VMEM((sp, 9 * ch, cells), BF16),
            pltpu.VMEM((6 * ch, 9 * ch), BF16),
            pltpu.VMEM((3 * ch, 9 * ch), BF16),
            pltpu.VMEM((6 * ch, 9 * ch), BF16),
            pltpu.VMEM((3 * ch, 9 * ch), BF16),
            pltpu.VMEM((2 * sp * ch, cells), BF16),
            pltpu.VMEM((sp * ch, cells), BF16),
            pltpu.VMEM((2 * n2 * rs, 9 * ch), F32),
            pltpu.VMEM((n2 * rs, 9 * ch), F32),
            pltpu.VMEM((n2 * rs, 9 * ch), F32),
            pltpu.VMEM((max(n2 - 1, 1), rs, 9 * ch), F32),
            pltpu.VMEM((2 * n2 * rs, 9 * ch), F32),
            dma((mb, sp)), dma, dma((mb, sp)),
            dma((2, mb)), dma((2, mb)), dma((2, mb)), dma((2, mb)),
            dma((mb, sp)), dma((mb, sp)), dma((mb, sp)),
            dma, dma, *[dma((rs // 8, n2))] * 6, dma,
        ],
        compiler_params=pltpu.CompilerParams(
            collective_id=0, has_side_effects=True, vmem_limit_bytes=60 * 1024 * 1024),
    )(act, filt, cotangent)
    return grads[None], fsum[None]


def solution(mesh):
    return jax.shard_map(
        functools.partial(per_device, mesh.shape["section"], mesh.shape["depth"]),
        mesh=mesh,
        in_specs=(
            P("section", None, "depth", None, None),
            P("section", None, None, None),
            P(None, "depth", None, None),
        ),
        out_specs=(P("section", None, "depth", None, None), P("section", None, None, None)),
        check_vma=False,
    )
```

time: 73.1 us -> 65 us (0.89)
  Pallas kernels: 67.3 us -> 61.4 us
  local copies, waits for them, and re-layouts: 4.95 us -> 2.86 us
    pallas_call x1, Pallas kernels: 67.3 us -> 61.4 us  [per_device(): pl.pallas_call(functools.partial(kernel, n_sec, n_dep, scale), out_shape=...]
    unnamed x8 -> x4, local copies, waits for them, and re-layouts: 4.95 us -> 2.86 us
where the time goes in v3:
time: 65 us; the launch traced here: 64.9 us
  Pallas kernels  61.4 us (94%)
  local copies, waits for them, and re-layouts  2.86 us (4%)
  between operations  0.65 us (1%)
    pallas_call x1, Pallas kernels, per_device(): pl.pallas_call(functools.partial(kernel, n_sec, n_dep, scale), out_shape=...  61.4 us
    unnamed x4, local copies, waits for them, and re-layouts  2.86 us

profile of v3, /device:TPU:1, one launch (start us, length us, event | category | flops | bytes accessed | tf_op | source)
XLA Modules:
  0.0 64.9 jit_solution(13343752685569226847)
XLA Ops:
  0.6 61.4 %shard_map.50 = (f32[4,2,64,256]{3,2,1,0:T(8,128)}, f32[27,64,64]{2,1,0:T(8,128)}) custom-call(f32[4,2,64,256]{3,2,1,0:T(8,128)} %bitcast.7, f32[27,64,64]{2,1,0:T(8,128)} %bitcast.5, f32[4,2,64,256]{3,2,1,0:T(8,128)} %cot.1), custom_call_target="tpu_custom_call" | custom-call | tf_op jit(solution)/shard_map/pallas_call | solution.py:391
  62.0 0.0 copy-start
  62.0 1.9 %copy.7 = f32[1,4,2,64,256]{4,3,2,1,0:T(8,128)} copy(f32[1,4,2,64,256]{4,3,2,1,0:T(8,128)} %bitcast.6) | data formatting | bytes 1048576
  64.0 0.0 copy-done
  64.0 0.9 %copy.8 = f32[1,27,64,64]{3,2,1,0:T(8,128)} copy(f32[1,27,64,64]{3,2,1,0:T(8,128)S(1)} %bitcast.4) | data formatting | bytes 884736
Async XLA Ops:
  62.0 2.0 %copy-start = (f32[27,64,64]{2,1,0:T(8,128)S(1)}, f32[27,64,64]{2,1,0:T(8,128)}, u32[]{:S(2)}) copy-start(f32[27,64,64]{2,1,0:T(8,128)} %get-tuple-element.5) | copy-start | bytes 1327108

commit v4 on v3

--- a/solution.py
+++ b/solution.py
@@ -155,13 +155,13 @@
         rows = rows_of(p, t)
         return remote(full.at[rows], full.at[rows], fw_send.at[p, t], fw_recv.at[p, t], partner)
 
+    @pl.when(has_outer)
+    def _():
+        for m in range(mb):
+            halo_out(m).start()
+
     for m in range(mb):
         halo_in(m).start()
-
-    @pl.when(has_outer)
-    def _():
-        for m in range(mb):
-            halo_out(m).start()
 
     @pl.when(jnp.logical_not(has_outer))
     def _():
@@ -244,24 +244,31 @@
             return carry
         lax.fori_loop(1, mb, more, 0)
 
+    def cotangents(m, d):
+        @pl.when(is_last)
+        def _():
+            cot_copy(m, d).wait()
+
+        @pl.when(jnp.logical_not(is_last))
+        def _():
+            hop(m, d).wait_recv()
+
+        s = up[m, d] * slope[m, d]
+        hi, lo = split(s)
+        r = sp - 1 - d
+        ss[2 * r * ch : (2 * r + 1) * ch, :] = hi
+        ss[(2 * r + 1) * ch : (2 * r + 2) * ch, :] = lo
+        sh[r * ch : (r + 1) * ch, :] = hi
+        put_patches(s, s_hi.at[d], s_lo.at[d], masks)
+
+    def inner(m):
+        cotangents(m, 0)
+        fsend[m, 0] = back(0, 0, 0)[0]
+        face_in(m).start()
+
+    inner(0)
+
     def step(m, carry):
-        def cotangents(d):
-            @pl.when(is_last)
-            def _():
-                cot_copy(m, d).wait()
-
-            @pl.when(jnp.logical_not(is_last))
-            def _():
-                hop(m, d).wait_recv()
-
-            s = up[m, d] * slope[m, d]
-            hi, lo = split(s)
-            r = sp - 1 - d
-            ss[2 * r * ch : (2 * r + 1) * ch, :] = hi
-            ss[(2 * r + 1) * ch : (2 * r + 2) * ch, :] = lo
-            sh[r * ch : (r + 1) * ch, :] = hi
-            put_patches(s, s_hi.at[d], s_lo.at[d], masks)
-
         def leave(j):
             @pl.when(sec > 0)
             def _():
@@ -269,11 +276,8 @@
 
             out_copy(m, j).start()
 
-        cotangents(0)
-        fsend[m, 0] = back(0, 0, 0)[0]
-        face_in(m).start()
         for d in range(1, sp):
-            cotangents(d)
+            cotangents(m, d)
         fsend[m, 1] = back(sp - 1, 2, 2)[0]
 
         @pl.when(has_outer)
@@ -309,6 +313,10 @@
         @pl.when(is_last & (m + 1 < mb))
         def _():
             prep(jnp.minimum(m + 1, mb - 1))
+
+        @pl.when(m + 1 < mb)
+        def _():
+            inner(jnp.minimum(m + 1, mb - 1))
 
         @pl.when(has_outer)
         def _():

time: 65 us -> 67.1 us (1.032)
  Pallas kernels: 61.4 us -> 63.4 us
    pallas_call x1, Pallas kernels: 61.4 us -> 63.4 us  [per_device(): pl.pallas_call(functools.partial(kernel, n_sec, n_dep, scale), out_shape=...]
where the time goes in v4:
time: 67.1 us; the launch traced here: 67 us
  Pallas kernels  63.4 us (94%)
  local copies, waits for them, and re-layouts  2.86 us (4%)
    pallas_call x1, Pallas kernels, per_device(): pl.pallas_call(functools.partial(kernel, n_sec, n_dep, scale), out_shape=...  63.4 us
    unnamed x4, local copies, waits for them, and re-layouts  2.86 us

profile of v4, /device:TPU:1, one launch (start us, length us, event | category | flops | bytes accessed | tf_op | source)
XLA Modules:
  0.0 67.0 jit_solution(7026796816971362114)
XLA Ops:
  0.6 63.4 %shard_map.50 = (f32[4,2,64,256]{3,2,1,0:T(8,128)}, f32[27,64,64]{2,1,0:T(8,128)}) custom-call(f32[4,2,64,256]{3,2,1,0:T(8,128)} %bitcast.7, f32[27,64,64]{2,1,0:T(8,128)} %bitcast.5, f32[4,2,64,256]{3,2,1,0:T(8,128)} %cot.1), custom_call_target="tpu_custom_call" | custom-call | tf_op jit(solution)/shard_map/pallas_call | solution.py:399
  64.1 0.0 copy-start
  64.1 1.9 %copy.7 = f32[1,4,2,64,256]{4,3,2,1,0:T(8,128)} copy(f32[1,4,2,64,256]{4,3,2,1,0:T(8,128)} %bitcast.6) | data formatting | bytes 1048576
  66.0 0.0 copy-done
  66.0 0.9 %copy.8 = f32[1,27,64,64]{3,2,1,0:T(8,128)} copy(f32[1,27,64,64]{3,2,1,0:T(8,128)S(1)} %bitcast.4) | data formatting | bytes 884736
Async XLA Ops:
  64.1 2.0 %copy-start = (f32[27,64,64]{2,1,0:T(8,128)S(1)}, f32[27,64,64]{2,1,0:T(8,128)}, u32[]{:S(2)}) copy-start(f32[27,64,64]{2,1,0:T(8,128)} %get-tuple-element.5) | copy-start | bytes 1327108

commit v5 on v4

--- a/solution.py
+++ b/solution.py
@@ -314,7 +314,7 @@
         def _():
             prep(jnp.minimum(m + 1, mb - 1))
 
-        @pl.when(m + 1 < mb)
+        @pl.when(is_last & (m + 1 < mb))
         def _():
             inner(jnp.minimum(m + 1, mb - 1))
 
@@ -324,6 +324,11 @@
 
         gbuf[m, sp - 1] = gbuf[m, sp - 1] + frecv[m, 1]
         leave(sp - 1)
+
+        @pl.when(jnp.logical_not(is_last) & (m + 1 < mb))
+        def _():
+            inner(jnp.minimum(m + 1, mb - 1))
+
         return carry
 
     lax.fori_loop(0, mb, step, 0)
@@ -433,7 +438,7 @@
             dma, dma, *[dma((rs // 8, n2))] * 6, dma,
         ],
         compiler_params=pltpu.CompilerParams(
-            collective_id=0, has_side_effects=True, vmem_limit_bytes=60 * 1024 * 1024),
+            collective_id=0, has_side_effects=True, vmem_limit_bytes=54000 * 1024),
     )(act, filt, cotangent)
     return grads[None], fsum[None]
 

time: 67.1 us -> 68 us (1.013)
    unnamed x4 -> x6, local copies, waits for them, and re-layouts: 2.86 us -> 3.29 us
where the time goes in v5:
time: 68 us; the launch traced here: 67.8 us
  Pallas kernels  63.9 us (94%)
  local copies, waits for them, and re-layouts  3.29 us (5%)
    pallas_call x1, Pallas kernels, per_device(): pl.pallas_call(functools.partial(kernel, n_sec, n_dep, scale), out_shape=...  63.9 us
    unnamed x6, local copies, waits for them, and re-layouts  3.29 us

profile of v5, /device:TPU:1, one launch (start us, length us, event | category | flops | bytes accessed | tf_op | source)
XLA Modules:
  0.0 67.8 jit_solution(17399623585027730315)
XLA Ops:
  0.6 0.0 copy-start
  0.6 1.0 %copy-done = f32[1,4,2,64,256]{4,3,2,1,0:T(8,128)S(1)} copy-done((f32[1,4,2,64,256]{4,3,2,1,0:T(8,128)S(1)}, f32[1,4,2,64,256]{4,3,2,1,0:T(8,128)}, u32[]{:S(2)}) %copy-start) | copy-done | bytes 524312
  1.7 63.9 %shard_map.50 = (f32[4,2,64,256]{3,2,1,0:T(8,128)S(1)}, f32[27,64,64]{2,1,0:T(8,128)}) custom-call(f32[4,2,64,256]{3,2,1,0:T(8,128)S(1)} %bitcast.5, f32[27,64,64]{2,1,0:T(8,128)} %bitcast.7, f32[4,2,64,256]{3,2,1,0:T(8,128)} %cot.1), custom_call_target="tpu_custom_call" | custom-call | tf_op jit(solution)/shard_map/pallas_call | solution.py:404
  65.6 0.0 copy-start.1
  65.6 0.8 %copy.7 = f32[1,4,2,64,256]{4,3,2,1,0:T(8,128)} copy(f32[1,4,2,64,256]{4,3,2,1,0:T(8,128)S(1)} %bitcast.4) | data formatting | bytes 1048576
  66.4 0.6 copy-done.1
  66.9 0.9 %copy.8 = f32[1,27,64,64]{3,2,1,0:T(8,128)} copy(f32[1,27,64,64]{3,2,1,0:T(8,128)S(1)} %bitcast.6) | data formatting | bytes 884736
Async XLA Ops:
  0.6 1.0 %copy-start = (f32[1,4,2,64,256]{4,3,2,1,0:T(8,128)S(1)}, f32[1,4,2,64,256]{4,3,2,1,0:T(8,128)}, u32[]{:S(2)}) copy-start(f32[1,4,2,64,256]{4,3,2,1,0:T(8,128)} %param.3) | copy-start | bytes 1572868
  65.6 1.4 %copy-start.1 = (f32[27,64,64]{2,1,0:T(8,128)S(1)}, f32[27,64,64]{2,1,0:T(8,128)}, u32[]{:S(2)}) copy-start(f32[27,64,64]{2,1,0:T(8,128)} %get-tuple-element.5) | copy-start | bytes 1327108
